TPU v7x, 128 devices: a whole 4x4x4 slice. The times are simulated.
128 devices in a mesh: fsdp: 16 (over z, x_hi, core), tp: 8 (over x_lo, y).
Axes of the slice: x: 4 (x_hi: 2, x_lo: 2; x = x_hi * 2 + x_lo), y: 4, z: 4, core: 2. Of those that a mesh axis runs over, the one named last changes fastest.
Arguments:
- hidden: bfloat16 [16384, 14336], P('fsdp', 'tp'), may hold values from -6 to 6
- grad_out: bfloat16 [16384, 4096], P('fsdp'), may hold values from -0.0625 to 0.0625
- master: float32 [4096, 14336], P('fsdp', 'tp'), may hold values from -0.046875 to 0.046875
- moment_one: float32 [4096, 14336], P('fsdp', 'tp'), may hold values from -3 to 3
- moment_two: float32 [4096, 14336], P('fsdp', 'tp'), may hold values from 0.1 to 4
Outputs:
- new_master: float32 [4096, 14336], P('fsdp', 'tp')
- new_one: float32 [4096, 14336], P('fsdp', 'tp')
- new_two: float32 [4096, 14336], P('fsdp', 'tp')
- quantized: bfloat16 [4096, 14336], P(None, 'fsdp')
- block_scales: bfloat16 [32, 112], P(None, 'fsdp')
All inputs are finite; a program needn't handle non-finite values.
Results may differ from a plain program's by a relative error of at most 0.0051.
Values may be sent and summed in bfloat16 or wider, within the bound.
A program may use at most 128 MiB of HBM per device.

v0:
```python
import jax
import jax.numpy as jnp
from jax import lax
from jax.sharding import PartitionSpec as P

BLOCK = 128


beta_one = 0.9
beta_two = 0.95
learn_rate = 0.005
adam_eps = 1e-08
scale_eps = 1e-06
steps_done = 4


def quantize(weights):
    rows, cols = weights.shape
    blocks = weights.reshape(rows // BLOCK, BLOCK, cols // BLOCK, BLOCK)
    peak = jnp.max(jnp.abs(blocks), axis=(1, 3)) + scale_eps
    scales = peak.astype(jnp.bfloat16)
    widened = lax.optimization_barrier(scales).astype(jnp.float32)
    values = (blocks / widened[:, None, :, None]).reshape(rows, cols).astype(jnp.bfloat16)
    return (values, scales)


def contract_tokens(left, right):
    return lax.dot_general(
        left, right, (((0,), (0,)), ((), ())), preferred_element_type=jnp.float32
    )


def local(hidden, grad_out, master, moment_one, moment_two):
    grad = lax.psum_scatter(
        contract_tokens(grad_out, hidden).astype(jnp.bfloat16),
        "fsdp",
        scatter_dimension=0,
        tiled=True,
    ).astype(jnp.float32)
    new_one = beta_one * moment_one + (1.0 - beta_one) * grad
    new_two = beta_two * moment_two + (1.0 - beta_two) * grad * grad
    fix_one = 1.0 - beta_one**steps_done
    fix_two = 1.0 - beta_two**steps_done
    new_master = master - learn_rate * (new_one / fix_one) / (
        jnp.sqrt(new_two / fix_two) + adam_eps
    )
    values, scales = quantize(new_master)
    wide_values, wide_scales = (
        lax.all_gather(values, "tp", axis=1, tiled=True),
        lax.all_gather(scales, "tp", axis=1, tiled=True),
    )
    quantized, block_scales = (
        lax.all_to_all(wide_values, "fsdp", split_axis=1, concat_axis=0, tiled=True),
        lax.all_to_all(wide_scales, "fsdp", split_axis=1, concat_axis=0, tiled=True),
    )
    return (new_master, new_one, new_two, quantized, block_scales)


def solution(mesh):
    return jax.shard_map(
        local,
        mesh=mesh,
        in_specs=(
            P("fsdp", "tp"),
            P("fsdp", None),
            P("fsdp", "tp"),
            P("fsdp", "tp"),
            P("fsdp", "tp"),
        ),
        out_specs=(
            P("fsdp", "tp"),
            P("fsdp", "tp"),
            P("fsdp", "tp"),
            P(None, "fsdp"),
            P(None, "fsdp"),
        ),
        check_vma=False,
    )
```

profile of v0, /device:TPU:0, one launch (start us, length us, event | category | flops | bytes accessed | tf_op | source)
XLA Modules:
  0.0 371.8 jit_solution(6424105375992613186)
XLA Ops:
  7.2 0.0 reduce-scatter.2.cloned.1.call-start
  7.2 22.1 %convolution_convert_fusion = bf16[4096,1792]{1,0:T(8,128)(2,1)} fusion(bf16[1024,4096]{1,0:T(8,128)(2,1)} %param.6, bf16[1024,1792]{1,0:T(8,128)(2,1)} %param.5), kind=kOutput, calls=%fused_computation | convolution fusion | flops 15039725568 | bytes 26738688 | tf_op jit(solution)/shard_map/dot_general | solution.py:28
  29.4 0.0 all-gather.3.cloned.1.call-start
  29.4 135.3 %reduce-scatter.2.cloned.1.call-done = bf16[256,1792]{1,0:T(8,128)(2,1)} async-done(((bf16[4096,1792]{1,0:T(8,128)(2,1)}), bf16[256,1792]{1,0:T(8,128)(2,1)}) %reduce-scatter.2.cloned.1.call-update) | async-done | bytes 917520 | tf_op jit(solution)/shard_map/reduce_scatter | solution.py:34
  164.7 6.1 %fusion.2 = (f32[256,1792]{1,0:T(8,128)}, f32[256,1792]{1,0:T(8,128)}, f32[256,1792]{1,0:T(8,128)}, f32[256,1792]{1,0:T(8,128)}) fusion(f32[256,1792]{1,0:T(8,128)S(1)} %copy-done, bf16[256,1792]{1,0:T(8,128)(2,1)} %reduce-scatter.2.cloned.1.call-done, f32[256,1792]{1,0:T(8,128)} %param.8, f32[256,1792]{1,0:T(8,128)} %param.9), kind=kLoop, calls=%fused_computation.10 | loop fusion | flops 6422528 | bytes 13762560 | tf_op jit(solution)/shard_map/abs | solution.py:20
  170.9 1.6 reshape.23
  172.5 0.2 reduce_max.9
  172.8 0.1 copy.26
  172.9 0.6 div.25
  173.4 0.1 copy.32
  173.6 1.7 copy.19
  175.2 3.2 divide_convert_fusion
  178.5 0.1 copy.21
  178.6 18.1 %all-gather = bf16[8,14,2]{1,2,0:T(2,128)(2,1)S(1)} all-gather(bf16[1,14,2]{1,2,0:T(2,128)(2,1)S(1)} %bitcast.30), channel_id=1, replica_groups=mesh['fsdp'=16,'tp'=8] {'tp'}, dimensions={0}, use_global_device_ids=true | all-gather | bytes 504 | tf_op jit(solution)/shard_map/all_gather | solution.py:50
  196.7 0.1 reshape.22
  196.8 0.1 all_to_all.32
  196.9 0.6 copy.23
  197.5 4.6 %all-to-all-start.1 = ((bf16[2,16,7]{2,0,1:T(2,128)(2,1)}), bf16[2,16,7]{2,0,1:T(2,128)(2,1)S(1)}, u32[]{:S(2)}, u32[]{:S(2)}) async-start(bf16[2,16,7]{2,0,1:T(2,128)(2,1)} %copy.23), calls=%async_computation.2 | async-start | bytes 16384 | tf_op jit(solution)/shard_map/all_to_all | solution.py:54
  202.1 56.7 %all-gather.3.cloned.1.call-done = bf16[256,14336]{1,0:T(8,128)(2,1)} async-done(((bf16[256,1792]{1,0:T(8,128)(2,1)}), bf16[256,14336]{1,0:T(8,128)(2,1)}) %all-gather.3.cloned.1.call-update) | async-done | bytes 7340048 | tf_op jit(solution)/shard_map/all_gather | solution.py:49
  258.8 7.2 %copy.31 = bf16[32,16,8,896]{3,2,0,1:T(8,128)(2,1)} copy(bf16[32,16,8,896]{3,2,1,0:T(8,128)(2,1)} %bitcast.26) | data formatting | bytes 14680064 | tf_op jit(solution)/shard_map/all_to_all | solution.py:53
  266.0 6.7 %all-to-all-start = ((bf16[256,16,896]{2,0,1:T(8,128)(2,1)}), bf16[256,16,896]{2,0,1:T(8,128)(2,1)}, u32[]{:S(2)}, u32[]{:S(2)}) async-start(bf16[256,16,896]{2,0,1:T(8,128)(2,1)} %bitcast.25), calls=%async_computation.1 | async-start | bytes 14680064 | tf_op jit(solution)/shard_map/all_to_all | solution.py:53
  272.7 0.7 copy.24
  273.4 84.8 %all-to-all-done = bf16[256,16,896]{2,0,1:T(8,128)(2,1)} async-done(((bf16[256,16,896]{2,0,1:T(8,128)(2,1)}), bf16[256,16,896]{2,0,1:T(8,128)(2,1)}, u32[]{:S(2)}, u32[]{:S(2)}) %all-to-all-start) | async-done | bytes 7340064 | tf_op jit(solution)/shard_map/all_to_all | solution.py:53
  358.2 6.7 %copy.34 = bf16[4096,896]{1,0:T(8,128)(2,1)} copy(bf16[4096,896]{1,0:T(8,128)(2,1)} %bitcast.1) | data formatting | bytes 14680064
  (8 shorter events, 0.1 us)
Async XLA Ops:
  7.2 157.6 %reduce-scatter.2.cloned.1.call-start = ((), (), s32[]{:S(2)}) async-start(), calls=%async_computation.3 | async-start | bytes 15597568 | tf_op jit(solution)/shard_map/reduce_scatter | solution.py:34
  29.3 135.4 %copy-start = (f32[256,1792]{1,0:T(8,128)S(1)}, f32[256,1792]{1,0:T(8,128)}, u32[]{:S(2)}) copy-start(f32[256,1792]{1,0:T(8,128)} %param.7) | copy-start | bytes 5505028
  29.4 229.4 %all-gather.3.cloned.1.call-start = ((), (), s32[]{:S(2)}) async-start(), calls=%async_computation.4 | async-start | bytes 8257536 | tf_op jit(solution)/shard_map/all_gather | solution.py:49
  197.5 68.5 %all-to-all-start.1 = ((bf16[2,16,7]{2,0,1:T(2,128)(2,1)}), bf16[2,16,7]{2,0,1:T(2,128)(2,1)S(1)}, u32[]{:S(2)}, u32[]{:S(2)}) async-start(bf16[2,16,7]{2,0,1:T(2,128)(2,1)} %copy.23), calls=%async_computation.2 | async-start | bytes 16384 | tf_op jit(solution)/shard_map/all_to_all | solution.py:54
  266.0 92.2 %all-to-all-start = ((bf16[256,16,896]{2,0,1:T(8,128)(2,1)}), bf16[256,16,896]{2,0,1:T(8,128)(2,1)}, u32[]{:S(2)}, u32[]{:S(2)}) async-start(bf16[256,16,896]{2,0,1:T(8,128)(2,1)} %bitcast.25), calls=%async_computation.1 | async-start | bytes 14680064 | tf_op jit(solution)/shard_map/all_to_all | solution.py:53
Sparse Core Ops, SparseCore 0:
  29.5 135.1 reduce-scatter.1
  178.6 80.1 all-gather.2
where the time goes:
time: 373 us; the launch traced here: 372 us
  waiting for transfers between devices  277 us (74%)
  matrix products  22.1 us (6%)
  local copies, waits for them, and re-layouts  19.6 us (5%)
  blocking collectives  18.1 us (5%)
  between operations  14.1 us (4%)
  starting transfers between devices  11.4 us (3%)
  other arithmetic  9.63 us (3%)
    reduce_scatter x1, waiting for transfers between devices, local(): lax.psum_scatter(contract_tokens(grad_out, hidden).astype(jnp.bfloat16),...  135 us
    all_to_all x1, waiting for transfers between devices, local(): lax.all_to_all(wide_values, 'fsdp', split_axis=1, concat_axis=0, tiled=True)  84.8 us
    all_gather x1, waiting for transfers between devices, local(): lax.all_gather(values, 'tp', axis=1, tiled=True)  56.7 us
    dot_general x1, matrix products, contract_tokens(): lax.dot_general(left, right, (((0,), (0,)), ((), ())), preferred_element_...  22.1 us
    all_gather x1, blocking collectives, local(): lax.all_gather(scales, 'tp', axis=1, tiled=True)  18.1 us
    unnamed x8, local copies, waits for them, and re-layouts  7.8 us
  transfers between devices with their start and end apart: 4, of which 3 were waited for; matrix products, arithmetic and copies ran while one was open for 2% of the time, Pallas kernels for 0%

commit v1 on v0

v1 whole, which is shorter than its diff:
```python
import functools

import jax
import jax.numpy as jnp
from jax import lax
from jax.experimental import pallas as pl
from jax.experimental.pallas import tpu as pltpu
from jax.sharding import PartitionSpec as P

beta_one = 0.9
beta_two = 0.95
learn_rate = 0.005
adam_eps = 1e-08
scale_eps = 1e-06
steps_done = 4

NC = 7
HALF = 896
F32 = jnp.float32
BF16 = jnp.bfloat16
MESH = pl.DeviceIdType.MESH


def kernel(
    hid_in, go_in, ma_in, m1_in, m2_in,
    ma_out, m1_out, m2_out, q_out, sc_out,
    hid, hidt, go, ma, m1, m2, gown, goth, crecv, z1, z2, own, xs, xr, qs, full, sacc, sfull,
    lsem, osem, qsem, csend, crcv, zsend, zrcv, xsend, xrcv, dsend, drcv,
    lsend, lrcv, ysend, yrcv, ssend, srcv,
):
    f = lax.axis_index("fsdp")
    t = lax.axis_index("tp")
    c = lax.rem(f, 2)
    g = f // 2
    xh = lax.rem(g, 2)
    z = g // 2
    y = lax.rem(t, 4)
    xl = t // 4
    zp, zm, zo = lax.rem(z + 1, 4), lax.rem(z + 3, 4), lax.rem(z + 2, 4)
    yp, ym, yo = lax.rem(y + 1, 4), lax.rem(y + 3, 4), lax.rem(y + 2, 4)
    dev_core = (f + 1 - 2 * c, t)
    dev_zp = (f + 4 * (zp - z), t)
    dev_zm = (f + 4 * (zm - z), t)
    dev_x = (f + 2 - 4 * xh, t)
    dev_l = (f, t + 4 - 8 * xl)
    dev_yp = (f, t + yp - y)
    dev_ym = (f, t + ym - y)
    piece = 2 * y + xl
    is_self = jnp.logical_and(g == t, piece // 4 == c)

    def target(h, i):
        j = 4 * c + i
        return (2 * t + h, lax.rem(j, 2) * 4 + j // 2)

    loads = [
        pltpu.make_async_copy(hid_in, hid, lsem.at[0]),
        pltpu.make_async_copy(go_in, go, lsem.at[1]),
        pltpu.make_async_copy(ma_in, ma, lsem.at[2]),
        pltpu.make_async_copy(m1_in, m1, lsem.at[3]),
        pltpu.make_async_copy(m2_in, m2, lsem.at[4]),
    ]
    for load in loads:
        load.start()

    barrier = pltpu.get_barrier_semaphore()
    for dev in (dev_core, dev_zp, dev_zm, dev_x, dev_l, dev_yp, dev_ym):
        pl.semaphore_signal(barrier, inc=1, device_id=dev, device_id_type=MESH)
    for h in range(2):
        for i in range(4):
            fd, td = target(h, i)

            @pl.when(jnp.logical_not(jnp.logical_and(fd == f, td == t)))
            def _():
                pl.semaphore_signal(barrier, inc=1, device_id=(fd, td), device_id_type=MESH)

    for gs in range(8):
        fs, ts = 2 * gs + piece // 4, g

        @pl.when(jnp.logical_not(jnp.logical_and(fs == f, ts == t)))
        def _():
            pl.semaphore_signal(barrier, inc=1, device_id=(fs, ts), device_id_type=MESH)

    @pl.when(is_self)
    def _():
        pl.semaphore_wait(barrier, 21)

    @pl.when(jnp.logical_not(is_self))
    def _():
        pl.semaphore_wait(barrier, 23)

    sacc[...] = jnp.zeros_like(sacc)
    for load in loads:
        load.wait()

    def rdma(src, dst, send, recv, dev):
        return pltpu.make_async_remote_copy(
            src_ref=src, dst_ref=dst, send_sem=send, recv_sem=recv, device_id=dev, device_id_type=MESH
        )

    def core_copy(k, i):
        return rdma(goth.at[k, i], crecv.at[k, i], csend.at[k], crcv.at[k], dev_core)

    def core_all(k):
        return rdma(goth.at[k], crecv.at[k], csend.at[k], crcv.at[k], dev_core)

    def z_copies(k):
        a, b = pl.ds(0, 128), pl.ds(128, 128)
        far, up, down = pl.ds(2 * zo, 2), pl.ds(2 * zp, 2), pl.ds(2 * zm, 2)
        return (
            rdma(gown.at[k, far, b], z1.at[k, 0], zsend.at[k, 0], zrcv.at[k, 0], dev_zp),
            rdma(gown.at[k, far, a], z1.at[k, 1], zsend.at[k, 1], zrcv.at[k, 1], dev_zm),
            rdma(gown.at[k, up, a], z2.at[k, 0, :, a], zsend.at[k, 2], zrcv.at[k, 2], dev_zp),
            rdma(gown.at[k, down, b], z2.at[k, 1, :, b], zsend.at[k, 3], zrcv.at[k, 3], dev_zm),
            rdma(gown.at[k, up, b], z2.at[k, 0, :, b], zsend.at[k, 4], zrcv.at[k, 4], dev_zp),
            rdma(gown.at[k, down, a], z2.at[k, 1, :, a], zsend.at[k, 5], zrcv.at[k, 5], dev_zm),
        )

    def x_copy(k):
        return rdma(xs.at[k], xr.at[k], xsend.at[k], xrcv.at[k], dev_x)

    def l_copy(k):
        rows = pl.ds(piece * 64, 64)
        return rdma(full.at[k, :, rows], full.at[k, :, rows], lsend.at[k], lrcv.at[k], dev_l)

    def y_copies(k):
        mine = pl.ds(y * 128, 128)
        below, above = pl.ds(ym * 128, 128), pl.ds(yp * 128, 128)
        lo, hi = pl.ds(0, 4), pl.ds(4, 4)
        return (
            rdma(full.at[k, :, mine], full.at[k, :, mine], ysend.at[k, 0], yrcv.at[k, 0], dev_yp),
            rdma(full.at[k, :, mine], full.at[k, :, mine], ysend.at[k, 1], yrcv.at[k, 1], dev_ym),
            rdma(full.at[k, lo, below], full.at[k, lo, below], ysend.at[k, 2], yrcv.at[k, 2], dev_yp),
            rdma(full.at[k, hi, above], full.at[k, hi, above], ysend.at[k, 3], yrcv.at[k, 3], dev_ym),
        )

    def sl_copy():
        mine = pl.ds(piece, 1)
        return rdma(sfull.at[:, mine], sfull.at[:, mine], ssend.at[1], srcv.at[1], dev_l)

    def sy_copies():
        mine = pl.ds(2 * y, 2)
        below, above = pl.ds(2 * ym, 2), pl.ds(2 * yp, 2)
        lo, hi = pl.ds(0, 4), pl.ds(4, 4)
        return (
            rdma(sfull.at[:, mine], sfull.at[:, mine], ssend.at[2], srcv.at[2], dev_yp),
            rdma(sfull.at[:, mine], sfull.at[:, mine], ssend.at[3], srcv.at[3], dev_ym),
            rdma(sfull.at[lo, below], sfull.at[lo, below], ssend.at[4], srcv.at[4], dev_yp),
            rdma(sfull.at[hi, above], sfull.at[hi, above], ssend.at[5], srcv.at[5], dev_ym),
        )

    def out_copies(k):
        copies = []
        for n, (src, dst) in enumerate(((ma, ma_out), (m1, m1_out), (m2, m2_out))):
            for h in range(2):
                cols = pl.ds(pl.multiple_of(h * HALF + k * 128, 128), 128)
                copies.append(pltpu.make_async_copy(src.at[:, cols], dst.at[:, cols], osem.at[k, 2 * n + h]))
        return copies

    def q_copy(k):
        cols = pl.ds(pl.multiple_of(k * 128, 128), 128)
        return pltpu.make_async_copy(full.at[k], q_out.at[:, :, cols], qsem.at[k])

    def s_matmul(k):
        first = pl.ds(pl.multiple_of(k * 128, 128), 128)
        second = pl.ds(pl.multiple_of(HALF + k * 128, 128), 128)
        hidt[pl.ds(0, 128), :] = hid[:, first].T
        hidt[pl.ds(128, 128), :] = hid[:, second].T

        def block(i, parity):
            cols = pl.ds(pl.multiple_of((2 * i + parity) * 256, 256), 256)
            return jnp.dot(hidt[...], go[:, cols], preferred_element_type=F32).astype(BF16)

        def other(i, _):
            goth[k, i] = block(i, 1 - c)
            core_copy(k, i).start()
            return 0

        def mine(i, _):
            gown[k, i] = block(i, c)
            return 0

        lax.fori_loop(0, 8, other, 0)
        lax.fori_loop(0, 8, mine, 0)

    def s_zstart(k):
        core_all(k).wait_recv()

        def add(i, _):
            gown[k, i] = (gown[k, i].astype(F32) + crecv[k, i].astype(F32)).astype(BF16)
            return 0

        lax.fori_loop(0, 8, add, 0)
        for copy in z_copies(k)[:4]:
            copy.start()

    def s_zmid(k):
        copies = z_copies(k)
        for n, (zi, rows) in enumerate(((zp, pl.ds(128, 128)), (zm, pl.ds(0, 128)))):
            copies[n].wait_recv()
            blocks = pl.ds(2 * zi, 2)
            gown[k, blocks, rows] = (gown[k, blocks, rows].astype(F32) + z1[k, n].astype(F32)).astype(BF16)
            copies[4 + n].start()

    def s_zend(k):
        for copy in z_copies(k)[2:]:
            copy.wait_recv()

        def total(q):
            return gown[k, 2 * z + q].astype(F32) + z2[k, 0, q].astype(F32) + z2[k, 1, q].astype(F32)

        xs[k] = total(1 - xh).astype(BF16)
        x_copy(k).start()
        own[...] = total(xh)

    def s_update(k):
        x_copy(k).wait_recv()
        fix_one = 1.0 - beta_one**steps_done
        fix_two = 1.0 - beta_two**steps_done
        for h in range(2):
            cols = pl.ds(pl.multiple_of(h * HALF + k * 128, 128), 128)
            for r in range(2):
                rows = pl.ds(r * 128, 128)
                grad_t = own[pl.ds(h * 128, 128), rows] + xr[k, pl.ds(h * 128, 128), rows].astype(F32)
                grad = grad_t.T
                new_one = beta_one * m1[rows, cols] + (1.0 - beta_one) * grad
                new_two = beta_two * m2[rows, cols] + (1.0 - beta_two) * grad * grad
                new_master = ma[rows, cols] - learn_rate * (new_one / fix_one) / (
                    jnp.sqrt(new_two / fix_two) + adam_eps
                )
                m1[rows, cols] = new_one
                m2[rows, cols] = new_two
                ma[rows, cols] = new_master
                peak = jnp.max(jnp.max(jnp.abs(new_master), axis=0, keepdims=True), axis=1, keepdims=True)
                scale = (peak + scale_eps).astype(BF16).astype(F32)
                qs[k, h, rows, :] = (new_master / scale).astype(BF16)
                row = lax.broadcasted_iota(jnp.int32, (8, 128), 0)
                lane = lax.broadcasted_iota(jnp.int32, (8, 128), 1)
                here = jnp.logical_and(row == r, lane == k)
                sacc[h] = jnp.where(here, jnp.broadcast_to(scale, (8, 128)), sacc[h])
        for copy in out_copies(k):
            copy.start()
        for h in range(2):
            for i in range(4):
                fd, td = target(h, i)
                j = 4 * c + i
                dst_rows = pl.ds(j * 64, 64)
                here = jnp.logical_and(fd == f, td == t)

                @pl.when(jnp.logical_not(here))
                def _():
                    rdma(
                        qs.at[k, h, pl.ds(i * 64, 64)], full.at[k, g, dst_rows], dsend.at[k], drcv.at[k], (fd, td)
                    ).start()

                @pl.when(here)
                def _():
                    full[k, g, dst_rows, :] = qs[k, h, pl.ds(i * 64, 64), :]

                @pl.when(k == NC - 1)
                def _():
                    @pl.when(jnp.logical_not(here))
                    def _():
                        rdma(sacc.at[h], sfull.at[g, j], ssend.at[0], srcv.at[0], (fd, td)).start()

                    @pl.when(here)
                    def _():
                        sfull[g, j] = sacc[h]

    def direct_wait(k, send):
        def wait(count):
            part = full.at[k, pl.ds(0, count), pl.ds(0, 64)]
            copy = rdma(part, part, dsend.at[k], drcv.at[k], dev_core)
            copy.wait_send() if send else copy.wait_recv()

        @pl.when(is_self)
        def _():
            wait(7)

        @pl.when(jnp.logical_not(is_self))
        def _():
            wait(8)

    def scale_direct_wait(send):
        def wait(count):
            part = sfull.at[pl.ds(0, count), 0]
            copy = rdma(part, part, ssend.at[0], srcv.at[0], dev_core)
            copy.wait_send() if send else copy.wait_recv()

        @pl.when(is_self)
        def _():
            wait(7)

        @pl.when(jnp.logical_not(is_self))
        def _():
            wait(8)

    def s_pair(k):
        direct_wait(k, False)
        l_copy(k).start()

        @pl.when(k == NC - 1)
        def _():
            scale_direct_wait(False)
            sl_copy().start()

    def s_ystart(k):
        l_copy(k).wait_recv()
        for copy in y_copies(k)[:2]:
            copy.start()

        @pl.when(k == NC - 1)
        def _():
            sl_copy().wait_recv()
            for copy in sy_copies()[:2]:
                copy.start()

    def s_yforward(k):
        copies = y_copies(k)
        for n in range(2):
            copies[n].wait_recv()
            copies[2 + n].start()

        @pl.when(k == NC - 1)
        def _():
            small = sy_copies()
            for n in range(2):
                small[n].wait_recv()
                small[2 + n].start()

    def s_store(k):
        for copy in y_copies(k)[2:]:
            copy.wait_recv()
        q_copy(k).start()

        @pl.when(k == NC - 1)
        def _():
            for copy in sy_copies()[2:]:
                copy.wait_recv()
            for gs in range(8):
                for cs in range(2):
                    sc_out[pl.ds(gs * 4 + cs * 2, 2), :] = sfull[gs, 4 * cs, pl.ds(0, 2), :]

    order = (
        (0, s_zstart),
        (1, s_zend),
        (-1, s_matmul),
        (0, s_zmid),
        (2, s_pair),
        (3, s_yforward),
        (1, s_update),
        (2, s_ystart),
        (4, s_store),
    )

    def step(n, _):
        for delay, stage in order:
            k = n - 1 - delay

            @pl.when(jnp.logical_and(k >= 0, k < NC))
            def _():
                stage(k)

        return 0

    lax.fori_loop(0, NC + 5, step, 0)

    def drain(k, _):
        core_all(k).wait_send()
        for copy in z_copies(k):
            copy.wait_send()
        x_copy(k).wait_send()
        direct_wait(k, True)
        l_copy(k).wait_send()
        for copy in y_copies(k):
            copy.wait_send()
        for copy in out_copies(k):
            copy.wait()
        q_copy(k).wait()
        return 0

    lax.fori_loop(0, NC, drain, 0)
    scale_direct_wait(True)
    sl_copy().wait_send()
    for copy in sy_copies():
        copy.wait_send()


def local(hidden, grad_out, master, moment_one, moment_two):
    weights = jax.ShapeDtypeStruct((256, 1792), F32)
    vmem = pltpu.VMEM
    dma = pltpu.SemaphoreType.DMA
    anyspace = pl.BlockSpec(memory_space=pl.ANY)
    new_master, new_one, new_two, quantized, scales = pl.pallas_call(
        kernel,
        out_shape=(
            weights,
            weights,
            weights,
            jax.ShapeDtypeStruct((8, 512, HALF), BF16),
            jax.ShapeDtypeStruct((32, 128), F32),
        ),
        in_specs=[anyspace] * 5,
        out_specs=(anyspace,) * 4 + (pl.BlockSpec(memory_space=pltpu.VMEM),),
        scratch_shapes=[
            vmem((1024, 1792), BF16),
            vmem((256, 1024), BF16),
            vmem((1024, 4096), BF16),
            vmem((256, 1792), F32),
            vmem((256, 1792), F32),
            vmem((256, 1792), F32),
            vmem((NC, 8, 256, 256), BF16),
            vmem((NC, 8, 256, 256), BF16),
            vmem((NC, 8, 256, 256), BF16),
            vmem((NC, 2, 2, 128, 256), BF16),
            vmem((NC, 2, 2, 256, 256), BF16),
            vmem((256, 256), F32),
            vmem((NC, 256, 256), BF16),
            vmem((NC, 256, 256), BF16),
            vmem((NC, 2, 256, 128), BF16),
            vmem((NC, 8, 512, 128), BF16),
            vmem((2, 8, 128), F32),
            vmem((8, 8, 8, 128), F32),
            dma((5,)),
            dma((NC, 6)),
            dma((NC,)),
            dma((NC,)), dma((NC,)),
            dma((NC, 6)), dma((NC, 6)),
            dma((NC,)), dma((NC,)),
            dma((NC,)), dma((NC,)),
            dma((NC,)), dma((NC,)),
            dma((NC, 4)), dma((NC, 4)),
            dma((6,)), dma((6,)),
        ],
        compiler_params=pltpu.CompilerParams(
            collective_id=0, has_side_effects=True, vmem_limit_bytes=63 * 1024 * 1024
        ),
    )(hidden, grad_out, master, moment_one, moment_two)
    return (
        new_master,
        new_one,
        new_two,
        quantized.reshape(4096, HALF),
        scales[:, :NC].astype(BF16),
    )


def solution(mesh):
    return jax.shard_map(
        local,
        mesh=mesh,
        in_specs=(
            P("fsdp", "tp"),
            P("fsdp", None),
            P("fsdp", "tp"),
            P("fsdp", "tp"),
            P("fsdp", "tp"),
        ),
        out_specs=(
            P("fsdp", "tp"),
            P("fsdp", "tp"),
            P("fsdp", "tp"),
            P(None, "fsdp"),
            P(None, "fsdp"),
        ),
        check_vma=False,
    )
```

time: 373 us -> 147 us (0.39)
  waiting for transfers between devices: 277 us -> 0 us
  Pallas kernels: 0 us -> 133 us
  matrix products: 22.1 us -> 0 us
  blocking collectives: 18.1 us -> 0 us
  between operations: 14.1 us -> 0.65 us
  starting transfers between devices: 11.4 us -> 0 us
  other arithmetic: 9.63 us -> 0 us
  local copies, waits for them, and re-layouts: 19.6 us -> 11.6 us
    reduce_scatter x1 -> x0, waiting for transfers between devices: 135 us -> none  [local(): lax.psum_scatter(contract_tokens(grad_out, hidden).astype(jnp.bfloat16),...]
    pallas_call x0 -> x1, Pallas kernels: none -> 133 us  [local(): pl.pallas_call(kernel, out_shape=(weights, weights, weights, jax.ShapeDty...]
    all_to_all x2 -> x0, waiting for transfers between devices: 84.8 us -> none  [the longest x1 84.8 us: local(): lax.all_to_all(wide_values, 'fsdp', split_axis=1, concat_axis=0, tiled=True)]
    all_gather x1 -> x0, waiting for transfers between devices: 56.7 us -> none  [local(): lax.all_gather(values, 'tp', axis=1, tiled=True)]
    dot_general x1 -> x0, matrix products: 22.1 us -> none  [contract_tokens(): lax.dot_general(left, right, (((0,), (0,)), ((), ())), preferred_element_...]
    all_gather x1 -> x0, blocking collectives: 18.1 us -> none  [local(): lax.all_gather(scales, 'tp', axis=1, tiled=True)]
    all_to_all x2 -> x0, starting transfers between devices: 11.3 us -> none  [the longest x1 6.69 us: local(): lax.all_to_all(wide_values, 'fsdp', split_axis=1, concat_axis=0, tiled=True)]
    all_to_all x3 -> x0, local copies, waits for them, and re-layouts: 7.93 us -> none  [the longest x1 7.22 us: local(): lax.all_to_all(wide_values, 'fsdp', split_axis=1, concat_axis=0, tiled=True)]
  transfers between devices with their start and end apart: 4 -> 0, of which waited for: 3 -> 0; matrix products, arithmetic and copies ran while one was open for 2% -> 0% of each run, Pallas kernels for 0% -> 0%
where the time goes in v1:
time: 147 us; the launch traced here: 146 us
  Pallas kernels  133 us (90%)
  local copies, waits for them, and re-layouts  11.6 us (8%)
    pallas_call x1, Pallas kernels, local(): pl.pallas_call(kernel, out_shape=(weights, weights, weights, jax.ShapeDty...  133 us
    unnamed x9, local copies, waits for them, and re-layouts  10.8 us

profile of v1, /device:TPU:0, one launch (start us, length us, event | category | flops | bytes accessed | tf_op | source)
XLA Modules:
  0.0 145.6 jit_solution(12080283240709439319)
XLA Ops:
  0.6 133.3 %shard_map.92 = (f32[256,1792]{1,0:T(8,128)}, f32[256,1792]{1,0:T(8,128)}, f32[256,1792]{1,0:T(8,128)}, bf16[8,512,896]{2,1,0:T(8,128)(2,1)}, f32[32,128]{1,0:T(8,128)}) custom-call(bf16[1024,1792]{1,0:T(8,128)(2,1)} %hid_in.1, bf16[1024,4096]{1,0:T(8,128)(2,1)} %go_in.1, f32[256,1792]{1,0:T(8,128)} %ma_in.1, f32[256,1792]{1,0:T(8,128)} %m1_in.1, ...), custom_call_target="tpu_custom_call" | custom-call | tf_op jit(solution)/shard_map/pallas_call | solution.py:393
  133.9 0.0 copy-start.1
  133.9 0.9 slice.7
  134.8 0.7 copy.10
  135.5 0.0 copy-start
  135.5 3.0 %copy.15 = f32[256,1792]{1,0:T(8,128)} copy(f32[256,1792]{1,0:T(8,128)} %get-tuple-element.25) | data formatting | bytes 3670016
  138.5 0.0 copy-done.1
  138.5 1.2 copy.16
  139.7 2.8 %copy.17 = f32[256,1792]{1,0:T(8,128)} copy(f32[256,1792]{1,0:T(8,128)} %get-tuple-element.27) | data formatting | bytes 3670016
  142.5 0.0 copy-done
  142.5 3.0 %copy.18 = bf16[4096,896]{1,0:T(8,128)(2,1)} copy(bf16[4096,896]{1,0:T(8,128)(2,1)S(1)} %bitcast.1) | data formatting | bytes 14680064
Async XLA Ops:
  133.9 4.5 %copy-start.1 = (f32[256,1792]{1,0:T(8,128)S(1)}, f32[256,1792]{1,0:T(8,128)}, u32[]{:S(2)}) copy-start(f32[256,1792]{1,0:T(8,128)} %get-tuple-element.26) | copy-start | bytes 5505028
  135.5 7.1 %copy-start = (bf16[8,512,896]{2,1,0:T(8,128)(2,1)S(1)}, bf16[8,512,896]{2,1,0:T(8,128)(2,1)}, u32[]{:S(2)}) copy-start(bf16[8,512,896]{2,1,0:T(8,128)(2,1)} %get-tuple-element.13) | copy-start | bytes 22020100

commit v2 on v1

--- a/solution.py
+++ b/solution.py
@@ -24,8 +24,8 @@
 def kernel(
     hid_in, go_in, ma_in, m1_in, m2_in,
     ma_out, m1_out, m2_out, q_out, sc_out,
-    hid, hidt, go, ma, m1, m2, gown, goth, crecv, z1, z2, own, xs, xr, qs, full, sacc, sfull,
-    lsem, osem, qsem, csend, crcv, zsend, zrcv, xsend, xrcv, dsend, drcv,
+    hid, hidt, go, ma, m1, m2, gown, goth, crecv, z1, z2, own, xs, xr, qs, w, full, sacc, ws, sfull,
+    lsem, gsem, osem, qsem, csend, crcv, zsend, zrcv, xsend, xrcv, wsend, wrcv, dsend, drcv,
     lsend, lrcv, ysend, yrcv, ssend, srcv,
 ):
     f = lax.axis_index("fsdp")
@@ -45,52 +45,63 @@
     dev_l = (f, t + 4 - 8 * xl)
     dev_yp = (f, t + yp - y)
     dev_ym = (f, t + ym - y)
-    piece = 2 * y + xl
-    is_self = jnp.logical_and(g == t, piece // 4 == c)
-
-    def target(h, i):
-        j = 4 * c + i
-        return (2 * t + h, lax.rem(j, 2) * 4 + j // 2)
-
+    xo = g // 4
+    is_self = xo == xl
+    mine_x = jnp.where(is_self, xh, 1 - xh)
+
+    def y_dev(d):
+        return (f, xl * 4 + lax.rem(y + d, 4))
+
+    def target(ys, h):
+        xd = jnp.where(xh == ys % 2, xl, 1 - xl)
+        return (2 * (xl * 4 + ys) + h, xd * 4 + y)
+
+    def go_load(b):
+        cols = pl.ds(pl.multiple_of(b * 256, 256), 256)
+        return pltpu.make_async_copy(go_in.at[:, cols], go.at[:, cols], gsem.at[b])
+
+    hid_load = pltpu.make_async_copy(hid_in, hid, lsem.at[0])
     loads = [
-        pltpu.make_async_copy(hid_in, hid, lsem.at[0]),
-        pltpu.make_async_copy(go_in, go, lsem.at[1]),
-        pltpu.make_async_copy(ma_in, ma, lsem.at[2]),
-        pltpu.make_async_copy(m1_in, m1, lsem.at[3]),
-        pltpu.make_async_copy(m2_in, m2, lsem.at[4]),
+        pltpu.make_async_copy(ma_in, ma, lsem.at[1]),
+        pltpu.make_async_copy(m1_in, m1, lsem.at[2]),
+        pltpu.make_async_copy(m2_in, m2, lsem.at[3]),
     ]
+    hid_load.start()
+    for parity in (1 - c, c):
+        for i in range(8):
+            go_load(2 * i + parity).start()
     for load in loads:
         load.start()
 
     barrier = pltpu.get_barrier_semaphore()
-    for dev in (dev_core, dev_zp, dev_zm, dev_x, dev_l, dev_yp, dev_ym):
+    for dev in (dev_core, dev_zp, dev_zm, dev_x, dev_l, y_dev(1), y_dev(2), y_dev(3)):
         pl.semaphore_signal(barrier, inc=1, device_id=dev, device_id_type=MESH)
-    for h in range(2):
-        for i in range(4):
-            fd, td = target(h, i)
+    for ys in range(4):
+        for h in range(2):
+            fd, td = target(ys, h)
 
             @pl.when(jnp.logical_not(jnp.logical_and(fd == f, td == t)))
             def _():
                 pl.semaphore_signal(barrier, inc=1, device_id=(fd, td), device_id_type=MESH)
 
-    for gs in range(8):
-        fs, ts = 2 * gs + piece // 4, g
-
-        @pl.when(jnp.logical_not(jnp.logical_and(fs == f, ts == t)))
-        def _():
-            pl.semaphore_signal(barrier, inc=1, device_id=(fs, ts), device_id_type=MESH)
+    for zs in range(4):
+        for cs in range(2):
+            fs, ts = 4 * zs + 2 * mine_x + cs, xo * 4 + y
+
+            @pl.when(jnp.logical_not(jnp.logical_and(fs == f, ts == t)))
+            def _():
+                pl.semaphore_signal(barrier, inc=1, device_id=(fs, ts), device_id_type=MESH)
 
     @pl.when(is_self)
     def _():
-        pl.semaphore_wait(barrier, 21)
+        pl.semaphore_wait(barrier, 22)
 
     @pl.when(jnp.logical_not(is_self))
     def _():
-        pl.semaphore_wait(barrier, 23)
+        pl.semaphore_wait(barrier, 24)
 
     sacc[...] = jnp.zeros_like(sacc)
-    for load in loads:
-        load.wait()
+    hid_load.wait()
 
     def rdma(src, dst, send, recv, dev):
         return pltpu.make_async_remote_copy(
@@ -118,35 +129,30 @@
     def x_copy(k):
         return rdma(xs.at[k], xr.at[k], xsend.at[k], xrcv.at[k], dev_x)
 
+    def spread_copy(k, d):
+        yd = lax.rem(y + d, 4)
+        return rdma(qs.at[k, :, pl.ds(yd * 64, 64)], w.at[k, y], wsend.at[k], wrcv.at[k], y_dev(d))
+
     def l_copy(k):
-        rows = pl.ds(piece * 64, 64)
-        return rdma(full.at[k, :, rows], full.at[k, :, rows], lsend.at[k], lrcv.at[k], dev_l)
+        part = full.at[k, :, mine_x, :, y]
+        return rdma(part, part, lsend.at[k], lrcv.at[k], dev_l)
 
     def y_copies(k):
-        mine = pl.ds(y * 128, 128)
-        below, above = pl.ds(ym * 128, 128), pl.ds(yp * 128, 128)
-        lo, hi = pl.ds(0, 4), pl.ds(4, 4)
-        return (
-            rdma(full.at[k, :, mine], full.at[k, :, mine], ysend.at[k, 0], yrcv.at[k, 0], dev_yp),
-            rdma(full.at[k, :, mine], full.at[k, :, mine], ysend.at[k, 1], yrcv.at[k, 1], dev_ym),
-            rdma(full.at[k, lo, below], full.at[k, lo, below], ysend.at[k, 2], yrcv.at[k, 2], dev_yp),
-            rdma(full.at[k, hi, above], full.at[k, hi, above], ysend.at[k, 3], yrcv.at[k, 3], dev_ym),
-        )
+        copies = []
+        for n, x in enumerate((mine_x, 1 - mine_x)):
+            part = full.at[k, :, x, :, y]
+            below, above = full.at[k, pl.ds(0, 2), x, :, ym], full.at[k, pl.ds(2, 2), x, :, yp]
+            copies += [
+                rdma(part, part, ysend.at[k, 4 * n], yrcv.at[k, 4 * n], dev_yp),
+                rdma(part, part, ysend.at[k, 4 * n + 1], yrcv.at[k, 4 * n + 1], dev_ym),
+                rdma(below, below, ysend.at[k, 4 * n + 2], yrcv.at[k, 4 * n + 2], dev_yp),
+                rdma(above, above, ysend.at[k, 4 * n + 3], yrcv.at[k, 4 * n + 3], dev_ym),
+            ]
+        return copies
 
     def sl_copy():
-        mine = pl.ds(piece, 1)
-        return rdma(sfull.at[:, mine], sfull.at[:, mine], ssend.at[1], srcv.at[1], dev_l)
-
-    def sy_copies():
-        mine = pl.ds(2 * y, 2)
-        below, above = pl.ds(2 * ym, 2), pl.ds(2 * yp, 2)
-        lo, hi = pl.ds(0, 4), pl.ds(4, 4)
-        return (
-            rdma(sfull.at[:, mine], sfull.at[:, mine], ssend.at[2], srcv.at[2], dev_yp),
-            rdma(sfull.at[:, mine], sfull.at[:, mine], ssend.at[3], srcv.at[3], dev_ym),
-            rdma(sfull.at[lo, below], sfull.at[lo, below], ssend.at[4], srcv.at[4], dev_yp),
-            rdma(sfull.at[hi, above], sfull.at[hi, above], ssend.at[5], srcv.at[5], dev_ym),
-        )
+        part = sfull.at[:, mine_x]
+        return rdma(part, part, ssend.at[2], srcv.at[2], dev_l)
 
     def out_copies(k):
         copies = []
@@ -158,28 +164,34 @@
 
     def q_copy(k):
         cols = pl.ds(pl.multiple_of(k * 128, 128), 128)
-        return pltpu.make_async_copy(full.at[k], q_out.at[:, :, cols], qsem.at[k])
-
-    def s_matmul(k):
+        return pltpu.make_async_copy(full.at[k], q_out.at[:, :, :, :, :, cols], qsem.at[k])
+
+    def block(k, b):
+        @pl.when(k == 0)
+        def _():
+            go_load(b).wait()
+
+        cols = pl.ds(pl.multiple_of(b * 256, 256), 256)
+        return jnp.dot(hidt[...], go[:, cols], preferred_element_type=F32).astype(BF16)
+
+    def s_other(k):
         first = pl.ds(pl.multiple_of(k * 128, 128), 128)
         second = pl.ds(pl.multiple_of(HALF + k * 128, 128), 128)
         hidt[pl.ds(0, 128), :] = hid[:, first].T
         hidt[pl.ds(128, 128), :] = hid[:, second].T
 
-        def block(i, parity):
-            cols = pl.ds(pl.multiple_of((2 * i + parity) * 256, 256), 256)
-            return jnp.dot(hidt[...], go[:, cols], preferred_element_type=F32).astype(BF16)
-
         def other(i, _):
-            goth[k, i] = block(i, 1 - c)
+            goth[k, i] = block(k, 2 * i + 1 - c)
             core_copy(k, i).start()
             return 0
 
+        lax.fori_loop(0, 8, other, 0)
+
+    def s_mine(k):
         def mine(i, _):
-            gown[k, i] = block(i, c)
+            gown[k, i] = block(k, 2 * i + c)
             return 0
 
-        lax.fori_loop(0, 8, other, 0)
         lax.fori_loop(0, 8, mine, 0)
 
     def s_zstart(k):
@@ -213,6 +225,11 @@
         own[...] = total(xh)
 
     def s_update(k):
+        @pl.when(k == 0)
+        def _():
+            for load in loads:
+                load.wait()
+
         x_copy(k).wait_recv()
         fix_one = 1.0 - beta_one**steps_done
         fix_two = 1.0 - beta_two**steps_done
@@ -239,36 +256,57 @@
                 sacc[h] = jnp.where(here, jnp.broadcast_to(scale, (8, 128)), sacc[h])
         for copy in out_copies(k):
             copy.start()
-        for h in range(2):
-            for i in range(4):
-                fd, td = target(h, i)
-                j = 4 * c + i
-                dst_rows = pl.ds(j * 64, 64)
+        for d in range(1, 4):
+            spread_copy(k, d).start()
+        w[k, y] = qs[k, :, pl.ds(pl.multiple_of(y * 64, 64), 64), :]
+
+        @pl.when(k == NC - 1)
+        def _():
+            for d in range(1, 4):
+                rdma(sacc, ws.at[y], ssend.at[0], srcv.at[0], y_dev(d)).start()
+            ws[y] = sacc[...]
+
+    def spread_all(k):
+        part = w.at[k, pl.ds(0, 3)]
+        return rdma(part, part, wsend.at[k], wrcv.at[k], dev_yp)
+
+    def spread_scales():
+        part = ws.at[pl.ds(0, 3)]
+        return rdma(part, part, ssend.at[0], srcv.at[0], dev_yp)
+
+    def s_move(k):
+        spread_all(k).wait_recv()
+
+        @pl.when(k == NC - 1)
+        def _():
+            spread_scales().wait_recv()
+
+        for ys in range(4):
+            for h in range(2):
+                fd, td = target(ys, h)
                 here = jnp.logical_and(fd == f, td == t)
 
                 @pl.when(jnp.logical_not(here))
                 def _():
-                    rdma(
-                        qs.at[k, h, pl.ds(i * 64, 64)], full.at[k, g, dst_rows], dsend.at[k], drcv.at[k], (fd, td)
-                    ).start()
+                    rdma(w.at[k, ys, h], full.at[k, z, xh, c, y], dsend.at[k], drcv.at[k], (fd, td)).start()
 
                 @pl.when(here)
                 def _():
-                    full[k, g, dst_rows, :] = qs[k, h, pl.ds(i * 64, 64), :]
+                    full[k, z, xh, c, y] = w[k, ys, h]
 
                 @pl.when(k == NC - 1)
                 def _():
                     @pl.when(jnp.logical_not(here))
                     def _():
-                        rdma(sacc.at[h], sfull.at[g, j], ssend.at[0], srcv.at[0], (fd, td)).start()
+                        rdma(ws.at[ys, h], sfull.at[z, xh, c], ssend.at[1], srcv.at[1], (fd, td)).start()
 
                     @pl.when(here)
                     def _():
-                        sfull[g, j] = sacc[h]
-
-    def direct_wait(k, send):
+                        sfull[z, xh, c] = ws[ys, h]
+
+    def move_wait(k, send):
         def wait(count):
-            part = full.at[k, pl.ds(0, count), pl.ds(0, 64)]
+            part = w.at[k].reshape(8, 64, 128).at[pl.ds(0, count)]
             copy = rdma(part, part, dsend.at[k], drcv.at[k], dev_core)
             copy.wait_send() if send else copy.wait_recv()
 
@@ -280,10 +318,10 @@
         def _():
             wait(8)
 
-    def scale_direct_wait(send):
+    def scale_move_wait(send):
         def wait(count):
-            part = sfull.at[pl.ds(0, count), 0]
-            copy = rdma(part, part, ssend.at[0], srcv.at[0], dev_core)
+            part = ws.reshape(8, 8, 128).at[pl.ds(0, count)]
+            copy = rdma(part, part, ssend.at[1], srcv.at[1], dev_core)
             copy.wait_send() if send else copy.wait_recv()
 
         @pl.when(is_self)
@@ -295,60 +333,58 @@
             wait(8)
 
     def s_pair(k):
-        direct_wait(k, False)
+        move_wait(k, False)
         l_copy(k).start()
-
-        @pl.when(k == NC - 1)
-        def _():
-            scale_direct_wait(False)
-            sl_copy().start()
-
-    def s_ystart(k):
-        l_copy(k).wait_recv()
         for copy in y_copies(k)[:2]:
             copy.start()
 
         @pl.when(k == NC - 1)
         def _():
+            scale_move_wait(False)
+            sl_copy().start()
+
+    def s_ymid(k):
+        copies = y_copies(k)
+        l_copy(k).wait_recv()
+        copies[4].start()
+        copies[5].start()
+        copies[0].wait_recv()
+        copies[2].start()
+        copies[1].wait_recv()
+        copies[3].start()
+
+    def s_yend(k):
+        copies = y_copies(k)
+        copies[4].wait_recv()
+        copies[6].start()
+        copies[5].wait_recv()
+        copies[7].start()
+
+    def s_store(k):
+        copies = y_copies(k)
+        for n in (2, 3, 6, 7):
+            copies[n].wait_recv()
+        q_copy(k).start()
+
+        @pl.when(k == NC - 1)
+        def _():
             sl_copy().wait_recv()
-            for copy in sy_copies()[:2]:
-                copy.start()
-
-    def s_yforward(k):
-        copies = y_copies(k)
-        for n in range(2):
-            copies[n].wait_recv()
-            copies[2 + n].start()
-
-        @pl.when(k == NC - 1)
-        def _():
-            small = sy_copies()
-            for n in range(2):
-                small[n].wait_recv()
-                small[2 + n].start()
-
-    def s_store(k):
-        for copy in y_copies(k)[2:]:
-            copy.wait_recv()
-        q_copy(k).start()
-
-        @pl.when(k == NC - 1)
-        def _():
-            for copy in sy_copies()[2:]:
-                copy.wait_recv()
-            for gs in range(8):
-                for cs in range(2):
-                    sc_out[pl.ds(gs * 4 + cs * 2, 2), :] = sfull[gs, 4 * cs, pl.ds(0, 2), :]
+            for zs in range(4):
+                for xs_ in range(2):
+                    for cs in range(2):
+                        sc_out[pl.ds(zs * 8 + xs_ * 4 + cs * 2, 2), :] = sfull[zs, xs_, cs, pl.ds(0, 2), :]
 
     order = (
         (0, s_zstart),
         (1, s_zend),
-        (-1, s_matmul),
+        (2, s_move),
+        (3, s_ymid),
+        (-1, s_other),
         (0, s_zmid),
+        (1, s_update),
         (2, s_pair),
-        (3, s_yforward),
-        (1, s_update),
-        (2, s_ystart),
+        (-1, s_mine),
+        (3, s_yend),
         (4, s_store),
     )
 
@@ -369,7 +405,8 @@
         for copy in z_copies(k):
             copy.wait_send()
         x_copy(k).wait_send()
-        direct_wait(k, True)
+        spread_all(k).wait_send()
+        move_wait(k, True)
         l_copy(k).wait_send()
         for copy in y_copies(k):
             copy.wait_send()
@@ -379,10 +416,9 @@
         return 0
 
     lax.fori_loop(0, NC, drain, 0)
-    scale_direct_wait(True)
+    spread_scales().wait_send()
+    scale_move_wait(True)
     sl_copy().wait_send()
-    for copy in sy_copies():
-        copy.wait_send()
 
 
 def local(hidden, grad_out, master, moment_one, moment_two):
@@ -396,7 +432,7 @@
             weights,
             weights,
             weights,
-            jax.ShapeDtypeStruct((8, 512, HALF), BF16),
+            jax.ShapeDtypeStruct((4, 2, 2, 4, 64, HALF), BF16),
             jax.ShapeDtypeStruct((32, 128), F32),
         ),
         in_specs=[anyspace] * 5,
@@ -417,10 +453,13 @@
             vmem((NC, 256, 256), BF16),
             vmem((NC, 256, 256), BF16),
             vmem((NC, 2, 256, 128), BF16),
-            vmem((NC, 8, 512, 128), BF16),
+            vmem((NC, 4, 2, 64, 128), BF16),
+            vmem((NC, 4, 2, 2, 4, 64, 128), BF16),
             vmem((2, 8, 128), F32),
-            vmem((8, 8, 8, 128), F32),
-            dma((5,)),
+            vmem((4, 2, 8, 128), F32),
+            vmem((4, 2, 2, 8, 128), F32),
+            dma((4,)),
+            dma((16,)),
             dma((NC, 6)),
             dma((NC,)),
             dma((NC,)), dma((NC,)),
@@ -428,8 +467,9 @@
             dma((NC,)), dma((NC,)),
             dma((NC,)), dma((NC,)),
             dma((NC,)), dma((NC,)),
-            dma((NC, 4)), dma((NC, 4)),
-            dma((6,)), dma((6,)),
+            dma((NC,)), dma((NC,)),
+            dma((NC, 8)), dma((NC, 8)),
+            dma((3,)), dma((3,)),
         ],
         compiler_params=pltpu.CompilerParams(
             collective_id=0, has_side_effects=True, vmem_limit_bytes=63 * 1024 * 1024

time: 147 us -> 140 us (0.952)
  Pallas kernels: 133 us -> 128 us
    pallas_call x1, Pallas kernels: 133 us -> 128 us  [local(): pl.pallas_call(kernel, out_shape=(weights, weights, weights, jax.ShapeDty...]
where the time goes in v2:
time: 140 us
  Pallas kernels  128 us (91%)
  local copies, waits for them, and re-layouts  11.6 us (8%)
    pallas_call x1, Pallas kernels, local(): pl.pallas_call(kernel, out_shape=(weights, weights, weights, jax.ShapeDty...  128 us
    unnamed x9, local copies, waits for them, and re-layouts  10.8 us

profile of v2, /device:TPU:0, one launch (start us, length us, event | category | flops | bytes accessed | tf_op | source)
XLA Modules:
  0.0 139.9 jit_solution(14183316725628407650)
XLA Ops:
  0.6 127.6 %shard_map.92 = (f32[256,1792]{1,0:T(8,128)}, f32[256,1792]{1,0:T(8,128)}, f32[256,1792]{1,0:T(8,128)}, bf16[4,2,2,4,64,896]{5,4,3,2,1,0:T(8,128)(2,1)}, f32[32,128]{1,0:T(8,128)}) custom-call(bf16[1024,1792]{1,0:T(8,128)(2,1)} %hid_in.1, bf16[1024,4096]{1,0:T(8,128)(2,1)} %go_in.1, f32[256,1792]{1,0:T(8,128)} %ma_in.1, f32[256,1792]{1,0:T(8,128)} %m1_in.1, ...), custom_call_target="tpu_custom_call" | custom-call | tf_op jit(solution)/shard_map/pallas_call | solution.py:429
  128.2 0.0 copy-start.1
  128.2 0.9 slice.7
  129.1 0.7 copy.10
  129.7 0.0 copy-start
  129.7 3.0 %copy.15 = f32[256,1792]{1,0:T(8,128)} copy(f32[256,1792]{1,0:T(8,128)} %get-tuple-element.25) | data formatting | bytes 3670016
  132.7 0.0 copy-done.1
  132.7 1.2 copy.16
  134.0 2.8 %copy.17 = f32[256,1792]{1,0:T(8,128)} copy(f32[256,1792]{1,0:T(8,128)} %get-tuple-element.27) | data formatting | bytes 3670016
  136.8 0.0 copy-done
  136.8 3.0 %copy.18 = bf16[4096,896]{1,0:T(8,128)(2,1)} copy(bf16[4096,896]{1,0:T(8,128)(2,1)S(1)} %bitcast.1) | data formatting | bytes 14680064
Async XLA Ops:
  128.2 4.5 %copy-start.1 = (f32[256,1792]{1,0:T(8,128)S(1)}, f32[256,1792]{1,0:T(8,128)}, u32[]{:S(2)}) copy-start(f32[256,1792]{1,0:T(8,128)} %get-tuple-element.26) | copy-start | bytes 5505028
  129.7 7.1 %copy-start = (bf16[4,2,2,4,64,896]{5,4,3,2,1,0:T(8,128)(2,1)S(1)}, bf16[4,2,2,4,64,896]{5,4,3,2,1,0:T(8,128)(2,1)}, u32[]{:S(2)}) copy-start(bf16[4,2,2,4,64,896]{5,4,3,2,1,0:T(8,128)(2,1)} %get-tuple-element.13) | copy-start | bytes 22020100

commit v3 on v2

--- a/solution.py
+++ b/solution.py
@@ -14,6 +14,7 @@
 scale_eps = 1e-06
 steps_done = 4
 
+NZ = 6
 NC = 7
 HALF = 896
 F32 = jnp.float32
@@ -23,8 +24,8 @@
 
 def kernel(
     hid_in, go_in, ma_in, m1_in, m2_in,
-    ma_out, m1_out, m2_out, q_out, sc_out,
-    hid, hidt, go, ma, m1, m2, gown, goth, crecv, z1, z2, own, xs, xr, qs, w, full, sacc, ws, sfull,
+    ma, m1, m2, full, sc_out,
+    hid, hidt, go, gown, goth, crecv, z1, z2, own, xs, xr, xf, qs, w, sacc, ws, sfull,
     lsem, gsem, osem, qsem, csend, crcv, zsend, zrcv, xsend, xrcv, wsend, wrcv, dsend, drcv,
     lsend, lrcv, ysend, yrcv, ssend, srcv,
 ):
@@ -126,6 +127,22 @@
             rdma(gown.at[k, down, a], z2.at[k, 1, :, a], zsend.at[k, 5], zrcv.at[k, 5], dev_zm),
         )
 
+    def zx_copies(k):
+        a, b = pl.ds(0, 128), pl.ds(128, 128)
+        far, up, down = 2 * zo + xh, 2 * zp + xh, 2 * zm + xh
+        return (
+            rdma(gown.at[k, far, b], z1.at[k, 0, 0], zsend.at[k, 0], zrcv.at[k, 0], dev_zp),
+            rdma(gown.at[k, far, a], z1.at[k, 1, 0], zsend.at[k, 1], zrcv.at[k, 1], dev_zm),
+            rdma(gown.at[k, up, a], z2.at[k, 0, 0, a], zsend.at[k, 2], zrcv.at[k, 2], dev_zp),
+            rdma(gown.at[k, down, b], z2.at[k, 1, 0, b], zsend.at[k, 3], zrcv.at[k, 3], dev_zm),
+            rdma(gown.at[k, up, b], z2.at[k, 0, 0, b], zsend.at[k, 4], zrcv.at[k, 4], dev_zp),
+            rdma(gown.at[k, down, a], z2.at[k, 1, 0, a], zsend.at[k, 5], zrcv.at[k, 5], dev_zm),
+        )
+
+    def xf_copy(k):
+        part = gown.reshape(NC, 4, 2, 256, 256).at[k, :, 1 - xh]
+        return rdma(part, xf.at[k - NZ], xsend.at[k], xrcv.at[k], dev_x)
+
     def x_copy(k):
         return rdma(xs.at[k], xr.at[k], xsend.at[k], xrcv.at[k], dev_x)
 
@@ -133,15 +150,20 @@
         yd = lax.rem(y + d, 4)
         return rdma(qs.at[k, :, pl.ds(yd * 64, 64)], w.at[k, y], wsend.at[k], wrcv.at[k], y_dev(d))
 
-    def l_copy(k):
-        part = full.at[k, :, mine_x, :, y]
-        return rdma(part, part, lsend.at[k], lrcv.at[k], dev_l)
+    def l_copies(k):
+        own_part = full.at[k, :, mine_x, :, y]
+        copies = [rdma(own_part, own_part, lsend.at[k, 0], lrcv.at[k, 0], dev_l)]
+        for n, yy in enumerate((ym, yp, yo)):
+            part = full.at[k, pl.ds(2, 2), mine_x, :, yy]
+            copies.append(rdma(part, part, lsend.at[k, n + 1], lrcv.at[k, n + 1], dev_l))
+        return copies
 
     def y_copies(k):
         copies = []
         for n, x in enumerate((mine_x, 1 - mine_x)):
-            part = full.at[k, :, x, :, y]
-            below, above = full.at[k, pl.ds(0, 2), x, :, ym], full.at[k, pl.ds(2, 2), x, :, yp]
+            size = 2 - n
+            part = full.at[k, pl.ds(0, 2 * size), x, :, y]
+            below, above = full.at[k, pl.ds(0, size), x, :, ym], full.at[k, pl.ds(size, size), x, :, yp]
             copies += [
                 rdma(part, part, ysend.at[k, 4 * n], yrcv.at[k, 4 * n], dev_yp),
                 rdma(part, part, ysend.at[k, 4 * n + 1], yrcv.at[k, 4 * n + 1], dev_ym),
@@ -166,35 +188,57 @@
         cols = pl.ds(pl.multiple_of(k * 128, 128), 128)
         return pltpu.make_async_copy(full.at[k], q_out.at[:, :, :, :, :, cols], qsem.at[k])
 
-    def block(k, b):
-        @pl.when(k == 0)
-        def _():
-            go_load(b).wait()
-
+    def block(b):
         cols = pl.ds(pl.multiple_of(b * 256, 256), 256)
         return jnp.dot(hidt[...], go[:, cols], preferred_element_type=F32).astype(BF16)
 
-    def s_other(k):
-        first = pl.ds(pl.multiple_of(k * 128, 128), 128)
-        second = pl.ds(pl.multiple_of(HALF + k * 128, 128), 128)
-        hidt[pl.ds(0, 128), :] = hid[:, first].T
-        hidt[pl.ds(128, 128), :] = hid[:, second].T
-
-        def other(i, _):
-            goth[k, i] = block(k, 2 * i + 1 - c)
-            core_copy(k, i).start()
-            return 0
-
-        lax.fori_loop(0, 8, other, 0)
-
-    def s_mine(k):
-        def mine(i, _):
-            gown[k, i] = block(k, 2 * i + c)
-            return 0
-
-        lax.fori_loop(0, 8, mine, 0)
-
-    def s_zstart(k):
+    def loaded(k, b):
+        @pl.when(k == 0)
+        def _():
+            go_load(b).wait()
+            go_load(b + 2).wait()
+
+    def s_piece(p):
+        n = p // 4
+        k = jnp.where(n == 2, NC - 1, jnp.where(n > 2, n - 1, n))
+        q = lax.rem(p, 4)
+
+        @pl.when(q == 0)
+        def _():
+            first = pl.ds(pl.multiple_of(k * 128, 128), 128)
+            second = pl.ds(pl.multiple_of(HALF + k * 128, 128), 128)
+            hidt[pl.ds(0, 128), :] = hid[:, first].T
+            hidt[pl.ds(128, 128), :] = hid[:, second].T
+
+        @pl.when(q < 2)
+        def _():
+            def other(j, _):
+                i = 4 * q + 2 * j
+                b = 2 * i + 1 - c
+                loaded(k, b)
+                one, two = block(b), block(b + 2)
+                goth[k, i] = one
+                goth[k, i + 1] = two
+                core_copy(k, i).start()
+                core_copy(k, i + 1).start()
+                return 0
+
+            lax.fori_loop(0, 2, other, 0)
+
+        @pl.when(q >= 2)
+        def _():
+            def mine(j, _):
+                i = 4 * (q - 2) + 2 * j
+                b = 2 * i + c
+                loaded(k, b)
+                one, two = block(b), block(b + 2)
+                gown[k, i] = one
+                gown[k, i + 1] = two
+                return 0
+
+            lax.fori_loop(0, 2, mine, 0)
+
+    def core_add(k):
         core_all(k).wait_recv()
 
         def add(i, _):
@@ -202,35 +246,95 @@
             return 0
 
         lax.fori_loop(0, 8, add, 0)
-        for copy in z_copies(k)[:4]:
-            copy.start()
+
+    def s_zstart(k):
+        @pl.when(k < NZ)
+        def _():
+            core_add(k)
+            for copy in z_copies(k)[:2]:
+                copy.start()
+
+        @pl.when(k >= NZ)
+        def _():
+            xf_copy(k).wait_recv()
+
+            def add(i, _):
+                b = 2 * i + xh
+                gown[k, b] = (gown[k, b].astype(F32) + xf[k - NZ, i].astype(F32)).astype(BF16)
+                return 0
+
+            lax.fori_loop(0, 4, add, 0)
+            for copy in zx_copies(k)[:2]:
+                copy.start()
+
+    def s_xsend(k):
+        core_add(k)
+        xf_copy(k).start()
+
+    def s_zfill(k):
+        @pl.when(k < NZ)
+        def _():
+            for copy in z_copies(k)[2:4]:
+                copy.start()
+
+        @pl.when(k >= NZ)
+        def _():
+            for copy in zx_copies(k)[2:4]:
+                copy.start()
 
     def s_zmid(k):
-        copies = z_copies(k)
-        for n, (zi, rows) in enumerate(((zp, pl.ds(128, 128)), (zm, pl.ds(0, 128)))):
-            copies[n].wait_recv()
-            blocks = pl.ds(2 * zi, 2)
-            gown[k, blocks, rows] = (gown[k, blocks, rows].astype(F32) + z1[k, n].astype(F32)).astype(BF16)
-            copies[4 + n].start()
+        sides = ((zp, pl.ds(128, 128)), (zm, pl.ds(0, 128)))
+
+        @pl.when(k < NZ)
+        def _():
+            copies = z_copies(k)
+            for n, (zi, rows) in enumerate(sides):
+                copies[n].wait_recv()
+                blocks = pl.ds(2 * zi, 2)
+                gown[k, blocks, rows] = (gown[k, blocks, rows].astype(F32) + z1[k, n].astype(F32)).astype(BF16)
+                copies[4 + n].start()
+
+        @pl.when(k >= NZ)
+        def _():
+            copies = zx_copies(k)
+            for n, (zi, rows) in enumerate(sides):
+                copies[n].wait_recv()
+                b = 2 * zi + xh
+                gown[k, b, rows] = (gown[k, b, rows].astype(F32) + z1[k, n, 0].astype(F32)).astype(BF16)
+                copies[4 + n].start()
 
     def s_zend(k):
-        for copy in z_copies(k)[2:]:
-            copy.wait_recv()
-
-        def total(q):
-            return gown[k, 2 * z + q].astype(F32) + z2[k, 0, q].astype(F32) + z2[k, 1, q].astype(F32)
-
-        xs[k] = total(1 - xh).astype(BF16)
-        x_copy(k).start()
-        own[...] = total(xh)
+        def total(q, slot):
+            return gown[k, 2 * z + q].astype(F32) + z2[k, 0, slot].astype(F32) + z2[k, 1, slot].astype(F32)
+
+        @pl.when(k < NZ)
+        def _():
+            for copy in z_copies(k)[2:]:
+                copy.wait_recv()
+            xs[k] = total(1 - xh, 1 - xh).astype(BF16)
+            x_copy(k).start()
+            own[...] = total(xh, xh)
+
+        @pl.when(k >= NZ)
+        def _():
+            for copy in zx_copies(k)[2:]:
+                copy.wait_recv()
+            own[...] = total(xh, 0)
+            xr[k] = jnp.zeros_like(xr[k])
+            update(k)
 
     def s_update(k):
+        @pl.when(k < NZ)
+        def _():
+            x_copy(k).wait_recv()
+            update(k)
+
+    def update(k):
         @pl.when(k == 0)
         def _():
             for load in loads:
                 load.wait()
 
-        x_copy(k).wait_recv()
         fix_one = 1.0 - beta_one**steps_done
         fix_two = 1.0 - beta_two**steps_done
         for h in range(2):
@@ -254,8 +358,6 @@
                 lane = lax.broadcasted_iota(jnp.int32, (8, 128), 1)
                 here = jnp.logical_and(row == r, lane == k)
                 sacc[h] = jnp.where(here, jnp.broadcast_to(scale, (8, 128)), sacc[h])
-        for copy in out_copies(k):
-            copy.start()
         for d in range(1, 4):
             spread_copy(k, d).start()
         w[k, y] = qs[k, :, pl.ds(pl.multiple_of(y * 64, 64), 64), :]
@@ -334,9 +436,9 @@
 
     def s_pair(k):
         move_wait(k, False)
-        l_copy(k).start()
         for copy in y_copies(k)[:2]:
             copy.start()
+        l_copies(k)[0].start()
 
         @pl.when(k == NC - 1)
         def _():
@@ -345,26 +447,30 @@
 
     def s_ymid(k):
         copies = y_copies(k)
-        l_copy(k).wait_recv()
+        pairs = l_copies(k)
+        pairs[0].wait_recv()
         copies[4].start()
         copies[5].start()
-        copies[0].wait_recv()
-        copies[2].start()
-        copies[1].wait_recv()
-        copies[3].start()
+        for n in range(2):
+            copies[n].wait_recv()
+            copies[2 + n].start()
+            pairs[1 + n].start()
 
     def s_yend(k):
         copies = y_copies(k)
-        copies[4].wait_recv()
-        copies[6].start()
-        copies[5].wait_recv()
-        copies[7].start()
+        for n in (4, 5):
+            copies[n].wait_recv()
+            copies[2 + n].start()
+        copies[2].wait_recv()
+        copies[3].wait_recv()
+        l_copies(k)[3].start()
 
     def s_store(k):
         copies = y_copies(k)
-        for n in (2, 3, 6, 7):
+        for n in (6, 7):
             copies[n].wait_recv()
-        q_copy(k).start()
+        for copy in l_copies(k)[1:]:
+            copy.wait_recv()
 
         @pl.when(k == NC - 1)
         def _():
@@ -376,21 +482,51 @@
 
     order = (
         (0, s_zstart),
-        (1, s_zend),
-        (2, s_move),
-        (3, s_ymid),
-        (-1, s_other),
-        (0, s_zmid),
-        (1, s_update),
-        (2, s_pair),
-        (-1, s_mine),
-        (3, s_yend),
-        (4, s_store),
+        (1, s_zmid),
+        (0, s_zfill),
+        (2, s_zend),
+        s_xsend,
+        2,
+        (5, s_ymid),
+        2,
+        (3, s_move),
+        (4, s_pair),
+        (6, s_store),
+        2,
+        (2, s_update),
+        (5, s_yend),
     )
 
+    def first(p, _):
+        s_piece(p)
+        return 0
+
+    lax.fori_loop(0, 4, first, 0)
+
     def step(n, _):
-        for delay, stage in order:
-            k = n - 1 - delay
+        ahead = 0
+        for entry in order:
+            if isinstance(entry, int):
+                def some(m, _, start=4 + 6 * n + ahead):
+                    @pl.when(start + m < 4 * NC)
+                    def _():
+                        s_piece(start + m)
+
+                    return 0
+
+                lax.fori_loop(0, entry, some, 0)
+                ahead += entry
+                continue
+            if entry is s_xsend:
+                for k, start in ((NC - 1, 2),):
+
+                    @pl.when(n == start)
+                    def _():
+                        entry(k)
+
+                continue
+            delay, stage = entry
+            k = n - delay
 
             @pl.when(jnp.logical_and(k >= 0, k < NC))
             def _():
@@ -398,21 +534,29 @@
 
         return 0
 
-    lax.fori_loop(0, NC + 5, step, 0)
+    lax.fori_loop(0, NC + 6, step, 0)
 
     def drain(k, _):
         core_all(k).wait_send()
-        for copy in z_copies(k):
-            copy.wait_send()
-        x_copy(k).wait_send()
+
+        @pl.when(k < NZ)
+        def _():
+            for copy in z_copies(k):
+                copy.wait_send()
+            x_copy(k).wait_send()
+
+        @pl.when(k >= NZ)
+        def _():
+            for copy in zx_copies(k):
+                copy.wait_send()
+            xf_copy(k).wait_send()
+
         spread_all(k).wait_send()
         move_wait(k, True)
-        l_copy(k).wait_send()
+        for copy in l_copies(k):
+            copy.wait_send()
         for copy in y_copies(k):
             copy.wait_send()
-        for copy in out_copies(k):
-            copy.wait()
-        q_copy(k).wait()
         return 0
 
     lax.fori_loop(0, NC, drain, 0)
@@ -421,8 +565,26 @@
     sl_copy().wait_send()
 
 
+def store_kernel(ma, m1, m2, full, scales, ma_out, m1_out, m2_out, q_out, sc_out, sem):
+    copies = [
+        pltpu.make_async_copy(src, dst, sem.at[n])
+        for n, (src, dst) in enumerate(((ma, ma_out), (m1, m1_out), (m2, m2_out)))
+    ]
+    for k in range(NC):
+        copies.append(
+            pltpu.make_async_copy(
+                full.at[k].reshape(4096, 128), q_out.at[:, pl.ds(k * 128, 128)], sem.at[3 + k]
+            )
+        )
+    for copy in copies:
+        copy.start()
+    sc_out[...] = scales[...].T[:NC].astype(BF16)
+    for copy in copies:
+        copy.wait()
+
+
 def local(hidden, grad_out, master, moment_one, moment_two):
-    weights = jax.ShapeDtypeStruct((256, 1792), F32)
+    weights = pltpu.VMEM((256, 1792), F32)
     vmem = pltpu.VMEM
     dma = pltpu.SemaphoreType.DMA
     anyspace = pl.BlockSpec(memory_space=pl.ANY)
@@ -432,18 +594,15 @@
             weights,
             weights,
             weights,
-            jax.ShapeDtypeStruct((4, 2, 2, 4, 64, HALF), BF16),
-            jax.ShapeDtypeStruct((32, 128), F32),
+            pltpu.VMEM((NC, 4, 2, 2, 4, 64, 128), BF16),
+            pltpu.VMEM((32, 128), F32),
         ),
         in_specs=[anyspace] * 5,
-        out_specs=(anyspace,) * 4 + (pl.BlockSpec(memory_space=pltpu.VMEM),),
+        out_specs=(pl.BlockSpec(memory_space=pltpu.VMEM),) * 4 + (pl.BlockSpec(memory_space=pltpu.VMEM),),
         scratch_shapes=[
             vmem((1024, 1792), BF16),
             vmem((256, 1024), BF16),
             vmem((1024, 4096), BF16),
-            vmem((256, 1792), F32),
-            vmem((256, 1792), F32),
-            vmem((256, 1792), F32),
             vmem((NC, 8, 256, 256), BF16),
             vmem((NC, 8, 256, 256), BF16),
             vmem((NC, 8, 256, 256), BF16),
@@ -452,9 +611,9 @@
             vmem((256, 256), F32),
             vmem((NC, 256, 256), BF16),
             vmem((NC, 256, 256), BF16),
+            vmem((NC - NZ, 4, 256, 256), BF16),
             vmem((NC, 2, 256, 128), BF16),
             vmem((NC, 4, 2, 64, 128), BF16),
-            vmem((NC, 4, 2, 2, 4, 64, 128), BF16),
             vmem((2, 8, 128), F32),
             vmem((4, 2, 8, 128), F32),
             vmem((4, 2, 2, 8, 128), F32),
@@ -467,21 +626,30 @@
             dma((NC,)), dma((NC,)),
             dma((NC,)), dma((NC,)),
             dma((NC,)), dma((NC,)),
-            dma((NC,)), dma((NC,)),
+            dma((NC, 4)), dma((NC, 4)),
             dma((NC, 8)), dma((NC, 8)),
             dma((3,)), dma((3,)),
         ],
         compiler_params=pltpu.CompilerParams(
-            collective_id=0, has_side_effects=True, vmem_limit_bytes=63 * 1024 * 1024
+            collective_id=0, has_side_effects=True, vmem_limit_bytes=46 * 1024 * 1024
         ),
     )(hidden, grad_out, master, moment_one, moment_two)
-    return (
-        new_master,
-        new_one,
-        new_two,
-        quantized.reshape(4096, HALF),
-        scales[:, :NC].astype(BF16),
-    )
+    weights = jax.ShapeDtypeStruct((256, 1792), F32)
+    *big, scale = pl.pallas_call(
+        store_kernel,
+        out_shape=(
+            weights,
+            weights,
+            weights,
+            jax.ShapeDtypeStruct((4096, HALF), BF16),
+            jax.ShapeDtypeStruct((NC, 32), BF16),
+        ),
+        in_specs=[anyspace] * 4 + [pl.BlockSpec(memory_space=pltpu.VMEM)],
+        out_specs=(anyspace,) * 4 + (pl.BlockSpec(memory_space=pltpu.VMEM),),
+        scratch_shapes=[dma((3 + NC,))],
+        compiler_params=pltpu.CompilerParams(vmem_limit_bytes=1024 * 1024),
+    )(new_master, new_one, new_two, quantized, scales)
+    return (*big, scale.T)
 
 
 def solution(mesh):

time: 140 us -> 126 us (0.900)
  local copies, waits for them, and re-layouts: 11.6 us -> 0 us
  Pallas kernels: 128 us -> 126 us
    unnamed x9 -> x0, local copies, waits for them, and re-layouts: 10.8 us -> none
    pallas_call x1 -> x2, Pallas kernels: 128 us -> 126 us  [the longest x1 120 us: local(): pl.pallas_call(kernel, out_shape=(weights, weights, weights, pltpu.VMEM((...]
where the time goes in v3:
time: 126 us
  Pallas kernels  126 us (100%)
    pallas_call x1, Pallas kernels, local(): pl.pallas_call(kernel, out_shape=(weights, weights, weights, pltpu.VMEM((...  120 us
    pallas_call x1, Pallas kernels, local(): pl.pallas_call(store_kernel, out_shape=(weights, weights, weights, jax.Sh...  5.34 us

profile of v3, /device:TPU:0, one launch (start us, length us, event | category | flops | bytes accessed | tf_op | source)
XLA Modules:
  0.0 126.4 jit_solution(15588768755507196873)
XLA Ops:
  0.6 120.4 %shard_map.92 = (f32[256,1792]{1,0:T(8,128)S(1)}, f32[256,1792]{1,0:T(8,128)S(1)}, f32[256,1792]{1,0:T(8,128)S(1)}, bf16[7,4,2,2,4,64,128]{6,5,4,3,2,1,0:T(8,128)(2,1)S(1)}, f32[32,128]{1,0:T(8,128)S(1)}) custom-call(bf16[1024,1792]{1,0:T(8,128)(2,1)} %hid_in.1, bf16[1024,4096]{1,0:T(8,128)(2,1)} %go_in.1, f32[256,1792]{1,0:T(8,128)} %ma_in.1, ...), custom_call_target="tpu_custom_call" | custom-call | tf_op jit(solution)/shard_map/pallas_call | solution.py:591
  121.0 5.3 %shard_map.93 = (f32[256,1792]{1,0:T(8,128)}, f32[256,1792]{1,0:T(8,128)}, f32[256,1792]{1,0:T(8,128)}, bf16[4096,896]{1,0:T(8,128)(2,1)}, bf16[7,32]{1,0:T(8,128)(2,1)}) custom-call(f32[256,1792]{1,0:T(8,128)S(1)} %get-tuple-element.15.ma, f32[256,1792]{1,0:T(8,128)S(1)} %get-tuple-element.16.m1, f32[256,1792]{1,0:T(8,128)S(1)} %get-tuple-element.17.m2, ...), custom_call_target="tpu_custom_call" | custom-call | tf_op jit(solution)/shard_map/pallas_call | solution.py:638

commit v4 on v3

--- a/solution.py
+++ b/solution.py
@@ -14,8 +14,10 @@
 scale_eps = 1e-06
 steps_done = 4
 
-NZ = 6
-NC = 7
+NB = 7
+NC = 2 * NB
+NZ = NC - 2
+ZP = 2
 HALF = 896
 F32 = jnp.float32
 BF16 = jnp.bfloat16
@@ -26,7 +28,7 @@
     hid_in, go_in, ma_in, m1_in, m2_in,
     ma, m1, m2, full, sc_out,
     hid, hidt, go, gown, goth, crecv, z1, z2, own, xs, xr, xf, qs, w, sacc, ws, sfull,
-    lsem, gsem, osem, qsem, csend, crcv, zsend, zrcv, xsend, xrcv, wsend, wrcv, dsend, drcv,
+    lsem, hsem, gsem, csend, crcv, zsend, zrcv, xsend, xrcv, wsend, wrcv, dsend, drcv,
     lsend, lrcv, ysend, yrcv, ssend, srcv,
 ):
     f = lax.axis_index("fsdp")
@@ -61,18 +63,27 @@
         cols = pl.ds(pl.multiple_of(b * 256, 256), 256)
         return pltpu.make_async_copy(go_in.at[:, cols], go.at[:, cols], gsem.at[b])
 
-    hid_load = pltpu.make_async_copy(hid_in, hid, lsem.at[0])
+    def hid_load(n, h):
+        cols = pl.ds(pl.multiple_of(h * HALF + n * 128, 128), 128)
+        return pltpu.make_async_copy(hid_in.at[:, cols], hid.at[:, cols], hsem.at[n, h])
+
     loads = [
-        pltpu.make_async_copy(ma_in, ma, lsem.at[1]),
-        pltpu.make_async_copy(m1_in, m1, lsem.at[2]),
-        pltpu.make_async_copy(m2_in, m2, lsem.at[3]),
+        pltpu.make_async_copy(ma_in, ma, lsem.at[0]),
+        pltpu.make_async_copy(m1_in, m1, lsem.at[1]),
+        pltpu.make_async_copy(m2_in, m2, lsem.at[2]),
     ]
-    hid_load.start()
-    for parity in (1 - c, c):
-        for i in range(8):
-            go_load(2 * i + parity).start()
-    for load in loads:
-        load.start()
+
+    def start_go(b, _):
+        go_load(b).start()
+        return 0
+
+    def start_hid(n, _):
+        for h in range(2):
+            hid_load(n, h).start()
+        return 0
+
+    start_hid(0, 0)
+    lax.fori_loop(0, 16, start_go, 0)
 
     barrier = pltpu.get_barrier_semaphore()
     for dev in (dev_core, dev_zp, dev_zm, dev_x, dev_l, y_dev(1), y_dev(2), y_dev(3)):
@@ -102,7 +113,7 @@
         pl.semaphore_wait(barrier, 24)
 
     sacc[...] = jnp.zeros_like(sacc)
-    hid_load.wait()
+    lax.fori_loop(1, NB, start_hid, 0)
 
     def rdma(src, dst, send, recv, dev):
         return pltpu.make_async_remote_copy(
@@ -140,7 +151,7 @@
         )
 
     def xf_copy(k):
-        part = gown.reshape(NC, 4, 2, 256, 256).at[k, :, 1 - xh]
+        part = gown.reshape(NC, 4, 2, 256, 128).at[k, :, 1 - xh]
         return rdma(part, xf.at[k - NZ], xsend.at[k], xrcv.at[k], dev_x)
 
     def x_copy(k):
@@ -148,22 +159,22 @@
 
     def spread_copy(k, d):
         yd = lax.rem(y + d, 4)
-        return rdma(qs.at[k, :, pl.ds(yd * 64, 64)], w.at[k, y], wsend.at[k], wrcv.at[k], y_dev(d))
+        return rdma(qs.at[k, :, pl.ds(yd * 32, 32)], w.at[k, y], wsend.at[k], wrcv.at[k], y_dev(d))
 
     def l_copies(k):
         own_part = full.at[k, :, mine_x, :, y]
         copies = [rdma(own_part, own_part, lsend.at[k, 0], lrcv.at[k, 0], dev_l)]
         for n, yy in enumerate((ym, yp, yo)):
-            part = full.at[k, pl.ds(2, 2), mine_x, :, yy]
+            part = full.at[k, pl.ds(ZP, 4 - ZP), mine_x, :, yy]
             copies.append(rdma(part, part, lsend.at[k, n + 1], lrcv.at[k, n + 1], dev_l))
         return copies
 
     def y_copies(k):
         copies = []
         for n, x in enumerate((mine_x, 1 - mine_x)):
-            size = 2 - n
-            part = full.at[k, pl.ds(0, 2 * size), x, :, y]
-            below, above = full.at[k, pl.ds(0, size), x, :, ym], full.at[k, pl.ds(size, size), x, :, yp]
+            groups = pl.ds(0, (4, ZP)[n])
+            part = full.at[k, groups, x, :, y]
+            below, above = full.at[k, groups, x, 0, ym], full.at[k, groups, x, 1, yp]
             copies += [
                 rdma(part, part, ysend.at[k, 4 * n], yrcv.at[k, 4 * n], dev_yp),
                 rdma(part, part, ysend.at[k, 4 * n + 1], yrcv.at[k, 4 * n + 1], dev_ym),
@@ -176,67 +187,59 @@
         part = sfull.at[:, mine_x]
         return rdma(part, part, ssend.at[2], srcv.at[2], dev_l)
 
-    def out_copies(k):
-        copies = []
-        for n, (src, dst) in enumerate(((ma, ma_out), (m1, m1_out), (m2, m2_out))):
-            for h in range(2):
-                cols = pl.ds(pl.multiple_of(h * HALF + k * 128, 128), 128)
-                copies.append(pltpu.make_async_copy(src.at[:, cols], dst.at[:, cols], osem.at[k, 2 * n + h]))
-        return copies
-
-    def q_copy(k):
-        cols = pl.ds(pl.multiple_of(k * 128, 128), 128)
-        return pltpu.make_async_copy(full.at[k], q_out.at[:, :, :, :, :, cols], qsem.at[k])
-
-    def block(b):
-        cols = pl.ds(pl.multiple_of(b * 256, 256), 256)
-        return jnp.dot(hidt[...], go[:, cols], preferred_element_type=F32).astype(BF16)
-
-    def loaded(k, b):
-        @pl.when(k == 0)
-        def _():
-            go_load(b).wait()
-            go_load(b + 2).wait()
+    def hid_wait(n, _):
+        for h in range(2):
+            hid_load(n, h).wait()
+        return 0
 
     def s_piece(p):
-        n = p // 4
-        k = jnp.where(n == 2, NC - 1, jnp.where(n > 2, n - 1, n))
-        q = lax.rem(p, 4)
+        n = p // 2
+        q = lax.rem(p, 2)
+        k = jnp.where(n < 4, n, jnp.where(n == 4, NZ, jnp.where(n == 5, 4, jnp.where(n == 6, NZ + 1, n - 2))))
+        kb = k // 2
+        row = lax.rem(k, 2) * 128
+
+        @pl.when(p == 0)
+        def _():
+            hid_wait(0, 0)
+
+        @pl.when(p == 2)
+        def _():
+            lax.fori_loop(1, NB, hid_wait, 0)
+            for load in loads:
+                load.start()
 
         @pl.when(q == 0)
         def _():
-            first = pl.ds(pl.multiple_of(k * 128, 128), 128)
-            second = pl.ds(pl.multiple_of(HALF + k * 128, 128), 128)
+            first = pl.ds(pl.multiple_of(kb * 128, 128), 128)
+            second = pl.ds(pl.multiple_of(HALF + kb * 128, 128), 128)
             hidt[pl.ds(0, 128), :] = hid[:, first].T
             hidt[pl.ds(128, 128), :] = hid[:, second].T
 
-        @pl.when(q < 2)
-        def _():
-            def other(j, _):
-                i = 4 * q + 2 * j
-                b = 2 * i + 1 - c
-                loaded(k, b)
-                one, two = block(b), block(b + 2)
-                goth[k, i] = one
-                goth[k, i + 1] = two
-                core_copy(k, i).start()
-                core_copy(k, i + 1).start()
-                return 0
-
-            lax.fori_loop(0, 2, other, 0)
-
-        @pl.when(q >= 2)
-        def _():
-            def mine(j, _):
-                i = 4 * (q - 2) + 2 * j
-                b = 2 * i + c
-                loaded(k, b)
-                one, two = block(b), block(b + 2)
-                gown[k, i] = one
-                gown[k, i + 1] = two
-                return 0
-
-            lax.fori_loop(0, 2, mine, 0)
+        def block(i):
+            far = pl.ds(pl.multiple_of((2 * i + 1 - c) * 256 + row, 128), 128)
+            near = pl.ds(pl.multiple_of((2 * i + c) * 256 + row, 128), 128)
+            both = jnp.concatenate([go[:, far], go[:, near]], axis=1)
+            return jnp.dot(hidt[...], both, preferred_element_type=F32).astype(BF16)
+
+        def pair(j, _):
+            i = 4 * q + 2 * j
+
+            @pl.when(k == 0)
+            def _():
+                for b in range(4):
+                    go_load(2 * i + b).wait()
+
+            one, two = block(i), block(i + 1)
+            goth[k, i] = one[:, :128]
+            goth[k, i + 1] = two[:, :128]
+            gown[k, i] = one[:, 128:]
+            gown[k, i + 1] = two[:, 128:]
+            core_copy(k, i).start()
+            core_copy(k, i + 1).start()
+            return 0
+
+        lax.fori_loop(0, 2, pair, 0)
 
     def core_add(k):
         core_all(k).wait_recv()
@@ -313,13 +316,13 @@
                 copy.wait_recv()
             xs[k] = total(1 - xh, 1 - xh).astype(BF16)
             x_copy(k).start()
-            own[...] = total(xh, xh)
+            own[lax.rem(k, 2)] = total(xh, xh)
 
         @pl.when(k >= NZ)
         def _():
             for copy in zx_copies(k)[2:]:
                 copy.wait_recv()
-            own[...] = total(xh, 0)
+            own[lax.rem(k, 2)] = total(xh, 0)
             xr[k] = jnp.zeros_like(xr[k])
             update(k)
 
@@ -337,30 +340,31 @@
 
         fix_one = 1.0 - beta_one**steps_done
         fix_two = 1.0 - beta_two**steps_done
+        kb = k // 2
+        r = lax.rem(k, 2)
+        rows = pl.ds(pl.multiple_of(r * 128, 128), 128)
         for h in range(2):
-            cols = pl.ds(pl.multiple_of(h * HALF + k * 128, 128), 128)
-            for r in range(2):
-                rows = pl.ds(r * 128, 128)
-                grad_t = own[pl.ds(h * 128, 128), rows] + xr[k, pl.ds(h * 128, 128), rows].astype(F32)
-                grad = grad_t.T
-                new_one = beta_one * m1[rows, cols] + (1.0 - beta_one) * grad
-                new_two = beta_two * m2[rows, cols] + (1.0 - beta_two) * grad * grad
-                new_master = ma[rows, cols] - learn_rate * (new_one / fix_one) / (
-                    jnp.sqrt(new_two / fix_two) + adam_eps
-                )
-                m1[rows, cols] = new_one
-                m2[rows, cols] = new_two
-                ma[rows, cols] = new_master
-                peak = jnp.max(jnp.max(jnp.abs(new_master), axis=0, keepdims=True), axis=1, keepdims=True)
-                scale = (peak + scale_eps).astype(BF16).astype(F32)
-                qs[k, h, rows, :] = (new_master / scale).astype(BF16)
-                row = lax.broadcasted_iota(jnp.int32, (8, 128), 0)
-                lane = lax.broadcasted_iota(jnp.int32, (8, 128), 1)
-                here = jnp.logical_and(row == r, lane == k)
-                sacc[h] = jnp.where(here, jnp.broadcast_to(scale, (8, 128)), sacc[h])
+            cols = pl.ds(pl.multiple_of(h * HALF + kb * 128, 128), 128)
+            grad_t = own[lax.rem(k, 2), pl.ds(h * 128, 128), :] + xr[k, pl.ds(h * 128, 128), :].astype(F32)
+            grad = grad_t.T
+            new_one = beta_one * m1[rows, cols] + (1.0 - beta_one) * grad
+            new_two = beta_two * m2[rows, cols] + (1.0 - beta_two) * grad * grad
+            new_master = ma[rows, cols] - learn_rate * (new_one / fix_one) / (
+                jnp.sqrt(new_two / fix_two) + adam_eps
+            )
+            m1[rows, cols] = new_one
+            m2[rows, cols] = new_two
+            ma[rows, cols] = new_master
+            peak = jnp.max(jnp.max(jnp.abs(new_master), axis=0, keepdims=True), axis=1, keepdims=True)
+            scale = (peak + scale_eps).astype(BF16).astype(F32)
+            qs[k, h] = (new_master / scale).astype(BF16)
+            line = lax.broadcasted_iota(jnp.int32, (8, 128), 0)
+            lane = lax.broadcasted_iota(jnp.int32, (8, 128), 1)
+            here = jnp.logical_and(line == r, lane == kb)
+            sacc[h] = jnp.where(here, jnp.broadcast_to(scale, (8, 128)), sacc[h])
         for d in range(1, 4):
             spread_copy(k, d).start()
-        w[k, y] = qs[k, :, pl.ds(pl.multiple_of(y * 64, 64), 64), :]
+        w[k, y] = qs[k, :, pl.ds(pl.multiple_of(y * 32, 32), 32), :]
 
         @pl.when(k == NC - 1)
         def _():
@@ -408,7 +412,7 @@
 
     def move_wait(k, send):
         def wait(count):
-            part = w.at[k].reshape(8, 64, 128).at[pl.ds(0, count)]
+            part = w.at[k].reshape(8, 32, 128).at[pl.ds(0, count)]
             copy = rdma(part, part, dsend.at[k], drcv.at[k], dev_core)
             copy.wait_send() if send else copy.wait_recv()
 
@@ -448,13 +452,13 @@
     def s_ymid(k):
         copies = y_copies(k)
         pairs = l_copies(k)
-        pairs[0].wait_recv()
-        copies[4].start()
-        copies[5].start()
         for n in range(2):
             copies[n].wait_recv()
             copies[2 + n].start()
             pairs[1 + n].start()
+        pairs[0].wait_recv()
+        copies[4].start()
+        copies[5].start()
 
     def s_yend(k):
         copies = y_copies(k)
@@ -481,34 +485,39 @@
                         sc_out[pl.ds(zs * 8 + xs_ * 4 + cs * 2, 2), :] = sfull[zs, xs_, cs, pl.ds(0, 2), :]
 
     order = (
-        (0, s_zstart),
-        (1, s_zmid),
-        (0, s_zfill),
-        (2, s_zend),
+        (0, s_zstart, 0, NC),
+        (0, s_zfill, 0, NC),
+        (3, s_zend, 0, NC),
         s_xsend,
-        2,
-        (5, s_ymid),
-        2,
-        (3, s_move),
-        (4, s_pair),
-        (6, s_store),
-        2,
-        (2, s_update),
-        (5, s_yend),
+        (4, s_move, NZ, NC),
+        1,
+        (7, s_pair, 0, NZ),
+        (5, s_pair, NZ, NC),
+        1,
+        (1, s_zmid, 0, NC),
+        (8, s_ymid, 0, NZ),
+        (6, s_ymid, NZ, NC),
+        1,
+        (4, s_update, 0, NZ),
+        (5, s_move, 0, NZ),
+        (9, s_yend, 0, NZ),
+        (7, s_yend, NZ, NC),
+        (11, s_store, 0, NZ),
+        (9, s_store, NZ, NC),
     )
 
     def first(p, _):
         s_piece(p)
         return 0
 
-    lax.fori_loop(0, 4, first, 0)
+    lax.fori_loop(0, 2, first, 0)
 
     def step(n, _):
         ahead = 0
         for entry in order:
             if isinstance(entry, int):
-                def some(m, _, start=4 + 6 * n + ahead):
-                    @pl.when(start + m < 4 * NC)
+                def some(m, _, start=2 + 3 * n + ahead):
+                    @pl.when(start + m < 2 * NC)
                     def _():
                         s_piece(start + m)
 
@@ -518,23 +527,23 @@
                 ahead += entry
                 continue
             if entry is s_xsend:
-                for k, start in ((NC - 1, 2),):
+                for k, start in ((NZ, 4), (NZ + 1, 6)):
 
                     @pl.when(n == start)
                     def _():
                         entry(k)
 
                 continue
-            delay, stage = entry
+            delay, stage, least, end = entry
             k = n - delay
 
-            @pl.when(jnp.logical_and(k >= 0, k < NC))
+            @pl.when(jnp.logical_and(k >= least, k < end))
             def _():
                 stage(k)
 
         return 0
 
-    lax.fori_loop(0, NC + 6, step, 0)
+    lax.fori_loop(0, NC + 9, step, 0)
 
     def drain(k, _):
         core_all(k).wait_send()
@@ -573,12 +582,14 @@
     for k in range(NC):
         copies.append(
             pltpu.make_async_copy(
-                full.at[k].reshape(4096, 128), q_out.at[:, pl.ds(k * 128, 128)], sem.at[3 + k]
+                full.at[k].reshape(16, 128, 128),
+                q_out.at[:, k % 2, :, pl.ds(k // 2 * 128, 128)],
+                sem.at[3 + k],
             )
         )
     for copy in copies:
         copy.start()
-    sc_out[...] = scales[...].T[:NC].astype(BF16)
+    sc_out[...] = scales[...].T[:NB].astype(BF16)
     for copy in copies:
         copy.wait()
 
@@ -594,7 +605,7 @@
             weights,
             weights,
             weights,
-            pltpu.VMEM((NC, 4, 2, 2, 4, 64, 128), BF16),
+            pltpu.VMEM((NC, 4, 2, 2, 4, 32, 128), BF16),
             pltpu.VMEM((32, 128), F32),
         ),
         in_specs=[anyspace] * 5,
@@ -603,24 +614,23 @@
             vmem((1024, 1792), BF16),
             vmem((256, 1024), BF16),
             vmem((1024, 4096), BF16),
-            vmem((NC, 8, 256, 256), BF16),
-            vmem((NC, 8, 256, 256), BF16),
-            vmem((NC, 8, 256, 256), BF16),
-            vmem((NC, 2, 2, 128, 256), BF16),
-            vmem((NC, 2, 2, 256, 256), BF16),
-            vmem((256, 256), F32),
-            vmem((NC, 256, 256), BF16),
-            vmem((NC, 256, 256), BF16),
-            vmem((NC - NZ, 4, 256, 256), BF16),
-            vmem((NC, 2, 256, 128), BF16),
-            vmem((NC, 4, 2, 64, 128), BF16),
+            vmem((NC, 8, 256, 128), BF16),
+            vmem((NC, 8, 256, 128), BF16),
+            vmem((NC, 8, 256, 128), BF16),
+            vmem((NC, 2, 2, 128, 128), BF16),
+            vmem((NC, 2, 2, 256, 128), BF16),
+            vmem((2, 256, 128), F32),
+            vmem((NC, 256, 128), BF16),
+            vmem((NC, 256, 128), BF16),
+            vmem((NC - NZ, 4, 256, 128), BF16),
+            vmem((NC, 2, 128, 128), BF16),
+            vmem((NC, 4, 2, 32, 128), BF16),
             vmem((2, 8, 128), F32),
             vmem((4, 2, 8, 128), F32),
             vmem((4, 2, 2, 8, 128), F32),
-            dma((4,)),
+            dma((3,)),
+            dma((NB, 2)),
             dma((16,)),
-            dma((NC, 6)),
-            dma((NC,)),
             dma((NC,)), dma((NC,)),
             dma((NC, 6)), dma((NC, 6)),
             dma((NC,)), dma((NC,)),
@@ -635,21 +645,21 @@
         ),
     )(hidden, grad_out, master, moment_one, moment_two)
     weights = jax.ShapeDtypeStruct((256, 1792), F32)
-    *big, scale = pl.pallas_call(
+    *weights, quantized, scale = pl.pallas_call(
         store_kernel,
         out_shape=(
             weights,
             weights,
             weights,
-            jax.ShapeDtypeStruct((4096, HALF), BF16),
-            jax.ShapeDtypeStruct((NC, 32), BF16),
+            jax.ShapeDtypeStruct((16, 2, 128, HALF), BF16),
+            jax.ShapeDtypeStruct((NB, 32), BF16),
         ),
         in_specs=[anyspace] * 4 + [pl.BlockSpec(memory_space=pltpu.VMEM)],
         out_specs=(anyspace,) * 4 + (pl.BlockSpec(memory_space=pltpu.VMEM),),
         scratch_shapes=[dma((3 + NC,))],
         compiler_params=pltpu.CompilerParams(vmem_limit_bytes=1024 * 1024),
     )(new_master, new_one, new_two, quantized, scales)
-    return (*big, scale.T)
+    return (*weights, quantized.reshape(4096, HALF), scale.T)
 
 
 def solution(mesh):

time: 126 us -> 122 us (0.968)
  Pallas kernels: 126 us -> 121 us
    pallas_call x1, Pallas kernels: 120 us -> 115 us  [local(): pl.pallas_call(kernel, out_shape=(weights, weights, weights, pltpu.VMEM((...]
where the time goes in v4:
time: 122 us; the launch traced here: 121 us
  Pallas kernels  121 us (99%)
    pallas_call x1, Pallas kernels, local(): pl.pallas_call(kernel, out_shape=(weights, weights, weights, pltpu.VMEM((...  115 us
    pallas_call x1, Pallas kernels, local(): pl.pallas_call(store_kernel, out_shape=(weights, weights, weights, jax.Sh...  5.38 us

profile of v4, /device:TPU:0, one launch (start us, length us, event | category | flops | bytes accessed | tf_op | source)
XLA Modules:
  0.0 121.4 jit_solution(4821593598056215967)
XLA Ops:
  0.6 115.4 %shard_map.92 = (f32[256,1792]{1,0:T(8,128)S(1)}, f32[256,1792]{1,0:T(8,128)S(1)}, f32[256,1792]{1,0:T(8,128)S(1)}, bf16[14,4,2,2,4,32,128]{6,5,4,3,2,1,0:T(8,128)(2,1)S(1)}, f32[32,128]{1,0:T(8,128)S(1)}) custom-call(bf16[1024,1792]{1,0:T(8,128)(2,1)} %hid_in.1, bf16[1024,4096]{1,0:T(8,128)(2,1)} %go_in.1, f32[256,1792]{1,0:T(8,128)} %ma_in.1, ...), custom_call_target="tpu_custom_call" | custom-call | tf_op jit(solution)/shard_map/pallas_call | solution.py:602
  116.0 5.4 %shard_map.93 = (f32[256,1792]{1,0:T(8,128)}, f32[256,1792]{1,0:T(8,128)}, f32[256,1792]{1,0:T(8,128)}, bf16[16,2,128,896]{3,2,1,0:T(8,128)(2,1)}, bf16[7,32]{1,0:T(8,128)(2,1)}) custom-call(f32[256,1792]{1,0:T(8,128)S(1)} %get-tuple-element.15.ma, f32[256,1792]{1,0:T(8,128)S(1)} %get-tuple-element.16.m1, f32[256,1792]{1,0:T(8,128)S(1)} %get-tuple-element.17.m2, ...), custom_call_target="tpu_custom_call" | custom-call | tf_op jit(solution)/shard_map/pallas_call | solution.py:648

commit v5 on v4

--- a/solution.py
+++ b/solution.py
@@ -484,6 +484,28 @@
                     for cs in range(2):
                         sc_out[pl.ds(zs * 8 + xs_ * 4 + cs * 2, 2), :] = sfull[zs, xs_, cs, pl.ds(0, 2), :]
 
+    def s_drain(k):
+        core_all(k).wait_send()
+
+        @pl.when(k < NZ)
+        def _():
+            for copy in z_copies(k):
+                copy.wait_send()
+            x_copy(k).wait_send()
+
+        @pl.when(k >= NZ)
+        def _():
+            for copy in zx_copies(k):
+                copy.wait_send()
+            xf_copy(k).wait_send()
+
+        spread_all(k).wait_send()
+        move_wait(k, True)
+        for copy in l_copies(k):
+            copy.wait_send()
+        for copy in y_copies(k):
+            copy.wait_send()
+
     order = (
         (0, s_zstart, 0, NC),
         (0, s_zfill, 0, NC),
@@ -504,6 +526,8 @@
         (7, s_yend, NZ, NC),
         (11, s_store, 0, NZ),
         (9, s_store, NZ, NC),
+        (11, s_drain, 0, NZ),
+        (9, s_drain, NZ, NC),
     )
 
     def first(p, _):
@@ -545,30 +569,6 @@
 
     lax.fori_loop(0, NC + 9, step, 0)
 
-    def drain(k, _):
-        core_all(k).wait_send()
-
-        @pl.when(k < NZ)
-        def _():
-            for copy in z_copies(k):
-                copy.wait_send()
-            x_copy(k).wait_send()
-
-        @pl.when(k >= NZ)
-        def _():
-            for copy in zx_copies(k):
-                copy.wait_send()
-            xf_copy(k).wait_send()
-
-        spread_all(k).wait_send()
-        move_wait(k, True)
-        for copy in l_copies(k):
-            copy.wait_send()
-        for copy in y_copies(k):
-            copy.wait_send()
-        return 0
-
-    lax.fori_loop(0, NC, drain, 0)
     spread_scales().wait_send()
     scale_move_wait(True)
     sl_copy().wait_send()

time: 122 us -> 122 us (level)
  no operation moved by 1% of the time
where the time goes in v5:
time: 122 us; the launch traced here: 121 us
  Pallas kernels  121 us (99%)
    pallas_call x1, Pallas kernels, local(): pl.pallas_call(kernel, out_shape=(weights, weights, weights, pltpu.VMEM((...  115 us
    pallas_call x1, Pallas kernels, local(): pl.pallas_call(store_kernel, out_shape=(weights, weights, weights, jax.Sh...  5.38 us

profile of v5, /device:TPU:0, one launch (start us, length us, event | category | flops | bytes accessed | tf_op | source)
XLA Modules:
  0.0 121.4 jit_solution(2971194420149571208)
XLA Ops:
  0.6 115.4 %shard_map.92 = (f32[256,1792]{1,0:T(8,128)S(1)}, f32[256,1792]{1,0:T(8,128)S(1)}, f32[256,1792]{1,0:T(8,128)S(1)}, bf16[14,4,2,2,4,32,128]{6,5,4,3,2,1,0:T(8,128)(2,1)S(1)}, f32[32,128]{1,0:T(8,128)S(1)}) custom-call(bf16[1024,1792]{1,0:T(8,128)(2,1)} %hid_in.1, bf16[1024,4096]{1,0:T(8,128)(2,1)} %go_in.1, f32[256,1792]{1,0:T(8,128)} %ma_in.1, ...), custom_call_target="tpu_custom_call" | custom-call | tf_op jit(solution)/shard_map/pallas_call | solution.py:602
  116.0 5.4 %shard_map.93 = (f32[256,1792]{1,0:T(8,128)}, f32[256,1792]{1,0:T(8,128)}, f32[256,1792]{1,0:T(8,128)}, bf16[16,2,128,896]{3,2,1,0:T(8,128)(2,1)}, bf16[7,32]{1,0:T(8,128)(2,1)}) custom-call(f32[256,1792]{1,0:T(8,128)S(1)} %get-tuple-element.15.ma, f32[256,1792]{1,0:T(8,128)S(1)} %get-tuple-element.16.m1, f32[256,1792]{1,0:T(8,128)S(1)} %get-tuple-element.17.m2, ...), custom_call_target="tpu_custom_call" | custom-call | tf_op jit(solution)/shard_map/pallas_call | solution.py:648
